TPU v7x, 256 devices: a whole 4x4x8 slice. The times are simulated.
256 devices in a mesh: bead: 16 (over x, z_hi), space: 16 (over z_lo, y, core).
Axes of the slice: x: 4, y: 4, z: 8 (z_hi: 4, z_lo: 2; z = z_hi * 2 + z_lo), core: 2. Of those that a mesh axis runs over, the one named last changes fastest.
Arguments:
- positions: float32 [64, 3, 4096], P('bead', None, 'space'), may hold values from -1 to 17
- species: int32 [4096], P('space'), may hold values from 0 to 1
- neighbors: int32 [32, 4096], P(None, 'space'), may hold values from 0 to 383, as said below
- counts: int32 [4096], P('space'), may hold values from 1 to 32, as said below
- send_rows: int32 [2048], P('space'), may hold values from 0 to 255, as said below
- embed: float32 [2, 128], replicated, may hold values from -6 to 6
- w_radial: float32 [2, 8, 128], replicated, may hold values from -2 to 2
- w_msg: float32 [2, 128, 128], replicated, may hold values from -0.5 to 0.5
- w_upd: float32 [2, 128, 128], replicated, may hold values from -0.5 to 0.5
- w_out: float32 [128], replicated, may hold values from -0.5 to 0.5
Outputs:
- forces: float32 [64, 3, 4096], P('bead', None, 'space')
Inputs may be any that keep to these rules, and one draw needn't show every extreme that they name: `neighbors`: entry n < 256 is the domain's own row n; 256 + s is the s-th left ghost and 320 + s the s-th right ghost. `counts`: slots of an atom below its count are live, the others padding. `send_rows`: each domain's first 64 entries are a permutation of its rows 0 to 63, the next 64 a permutation of its rows 192 to 255.
All inputs are finite; a program needn't handle non-finite values.
Results may differ from a plain program's by a relative error of at most 0.0003.
Values sent between devices are 32-bit elements; how exact they have to be, the bound alone decides.
A program may use at most 64 MiB of HBM per device.

v0:
```python
from functools import partial

import jax
import jax.numpy as jnp
from jax import lax
from jax.sharding import PartitionSpec as P

PC = 16


exact_mode = lax.Precision.HIGHEST
spacing_floor = 0.01
radial_width = 0.2
radial_reach = 1.5
block_rows = 128


def with_halo(block, sides, width):
    for axis, dim in sides:
        count = lax.axis_size(axis)
        forward = [(i, i + 1) for i in range(count - 1)]
        forward.append((count - 1, 0))
        backward = [(target, source) for source, target in forward]
        low = lax.ppermute(
            lax.slice_in_dim(block, block.shape[dim] - width, None, axis=dim), axis, forward
        )
        high = lax.ppermute(lax.slice_in_dim(block, 0, width, axis=dim), axis, backward)
        block = jnp.concatenate([low, block, high], axis=dim)
    return block


def contraction(full_beads, reduced_beads):
    rowpos = jnp.arange(reduced_beads, dtype=jnp.float32)[:, None]
    colpos = jnp.arange(full_beads, dtype=jnp.float32)[None, :]
    phase_gap = rowpos / reduced_beads - colpos / full_beads
    running = jnp.ones_like(phase_gap)
    for harmonic in range(1, reduced_beads // 2):
        running = running + 2.0 * jnp.cos(2.0 * jnp.pi * harmonic * phase_gap)
    running = running + jnp.cos(jnp.pi * reduced_beads * phase_gap)
    return running / full_beads


def silu_slope(argument):
    sigmoid_part = jax.nn.sigmoid(argument)
    return sigmoid_part * (1.0 + argument * (1.0 - sigmoid_part))


def blocked(values, which_axis):
    dims_now = values.shape
    blocks = dims_now[which_axis] // block_rows
    reshaped = values.reshape(
        dims_now[:which_axis] + (blocks, block_rows) + dims_now[which_axis + 1 :]
    )
    return jnp.moveaxis(reshaped, which_axis, 0)


def unblocked(values, which_axis):
    moved_axes = jnp.moveaxis(values, 0, which_axis)
    dims_now = moved_axes.shape
    merged = (dims_now[which_axis] * dims_now[which_axis + 1],)
    return moved_axes.reshape(dims_now[:which_axis] + merged + dims_now[which_axis + 2 :])


def chooser_table(rows, extent):
    columns = lax.broadcasted_iota(jnp.int32, rows.shape + (extent,), rows.ndim)
    return (rows[..., None] == columns).astype(jnp.float32)


def block_message(lent_ext, radial_basis, live_slots, neighbor_rows, radial_map, edge_scale):
    radial_w = jnp.einsum("nbkr,nc->bkrc", radial_basis, radial_map, precision=exact_mode)
    chooser = chooser_table(neighbor_rows, lent_ext.shape[1])
    near_rows = jnp.einsum("kre,bec->bkrc", chooser, lent_ext, precision=exact_mode)
    return edge_scale * jnp.einsum(
        "bkrc,kr->brc", radial_w * near_rows, live_slots, precision=exact_mode
    )


def block_backward(state_pair, inputs, lent_ext, radial_map, edge_scale, want_features):
    grad_lent, grad_points = state_pair
    radial_basis, offsets, displace, distance, live_slots, neighbor_rows, grad_message = inputs
    radial_w = jnp.einsum("nbkr,nc->bkrc", radial_basis, radial_map, precision=exact_mode)
    chooser = chooser_table(neighbor_rows, lent_ext.shape[1])
    near_rows = jnp.einsum("kre,bec->bkrc", chooser, lent_ext, precision=exact_mode)
    weighted = edge_scale * live_slots[None, :, :, None] * grad_message[:, None]
    grad_radial = weighted * near_rows
    grad_basis = jnp.einsum("bkrc,nc->nbkr", grad_radial, radial_map, precision=exact_mode)
    grad_distance = jnp.sum(grad_basis * radial_basis * offsets, axis=0) * (-2.0 / radial_width)
    grad_displace = grad_distance[:, None] * displace / distance[:, None]
    grad_points = grad_points + jnp.einsum(
        "kre,bckr->bce", chooser, grad_displace, precision=exact_mode
    )
    if want_features:
        grad_near = weighted * radial_w
        grad_lent = grad_lent + jnp.einsum(
            "kre,bkrc->bec", chooser, grad_near, precision=exact_mode
        )
    return ((grad_lent, grad_points), -jnp.sum(grad_displace, axis=2))


def on_device(
    positions, species, neighbors, counts, send_rows, embed, w_radial, w_msg, w_upd, w_out
):
    full_dev = positions.shape[0]
    atom_count = positions.shape[2]
    beads_all = full_dev * lax.axis_size("bead")
    reduced_dev = PC // lax.axis_size("bead")
    bead_index = lax.axis_index("bead")
    contract_table = contraction(beads_all, PC)
    own_columns = lax.dynamic_slice_in_dim(contract_table, bead_index * full_dev, full_dev, 1)
    own_table = lax.dynamic_slice_in_dim(contract_table, bead_index * reduced_dev, reduced_dev, 0)
    weights = own_table
    reduced = jnp.einsum(
        "kj,jcn->kcn",
        weights,
        lax.all_gather(positions, "bead", axis=0, tiled=True),
        precision=exact_mode,
    )
    ghost_count = send_rows.shape[0] // 2
    domains = lax.axis_size("space")
    domain = lax.axis_index("space")
    selector = chooser_table(send_rows, atom_count)
    lent_points = jnp.einsum("ga,bca->bcg", selector, reduced, precision=exact_mode)
    lent_species = jnp.dot(selector, species.astype(jnp.float32), precision=exact_mode)
    lent_species = lent_species[None, None]
    outgoing = jnp.concatenate([lent_points, lent_species], axis=1)
    arrived = with_halo(outgoing, (("space", 2),), ghost_count)
    borrowed = jnp.concatenate(
        [arrived[:, :, :ghost_count], arrived[:, :, 3 * ghost_count :]], axis=2
    )
    left_shift = jnp.where(domain == 0, -float(domains), 0.0)
    right_shift = jnp.where(domain == domains - 1, float(domains), 0.0)
    ghost_slot = jnp.arange(2 * ghost_count, dtype=jnp.int32)
    box_shift = jnp.where(ghost_slot < ghost_count, left_shift, right_shift).astype(jnp.float32)
    ghost_points = borrowed[:, :3].at[:, 0].add(box_shift[None])
    ghost_species = borrowed[0, 3]
    ext_points = jnp.concatenate([reduced, ghost_points], axis=2)
    extent = ext_points.shape[2]
    blocks_rows = blocked(neighbors, 1)

    def pick_points(rows_block):
        chooser = chooser_table(rows_block, extent)
        return jnp.einsum("kre,bce->bckr", chooser, ext_points, precision=exact_mode)

    near_points = unblocked(lax.map(pick_points, blocks_rows), 3)
    displace = near_points - reduced[:, :, None, :]
    distance = jnp.sqrt(jnp.sum(displace * displace, axis=1) + spacing_floor)
    basis_count = w_radial.shape[1]
    centers = radial_reach * jnp.arange(basis_count, dtype=jnp.float32) / (basis_count - 1)
    offsets = (distance[None] - centers[:, None, None, None]) / radial_width
    radial_basis = jnp.exp(-offsets * offsets)
    slot_index = lax.broadcasted_iota(jnp.int32, neighbors.shape, 0)
    live_slots = (slot_index < counts[None, :]).astype(jnp.float32)
    edge_scale = neighbors.shape[0] ** (-0.5)
    kinds = jnp.arange(embed.shape[0], dtype=jnp.int32)
    own_onehot = (species[:, None] == kinds[None, :]).astype(jnp.float32)
    ghost_onehot = (ghost_species[:, None] == kinds.astype(jnp.float32)[None, :]).astype(
        jnp.float32
    )
    ext_onehot = jnp.concatenate([own_onehot, ghost_onehot], axis=0)
    hidden = jnp.dot(own_onehot, embed, precision=exact_mode)[None]
    first_table = jnp.dot(embed, w_msg[0], precision=exact_mode)
    blocks_basis = blocked(radial_basis, 3)
    blocks_offsets = blocked(offsets, 3)
    blocks_displace = blocked(displace, 3)
    blocks_distance = blocked(distance, 2)
    blocks_live = blocked(live_slots, 1)
    layer_total = w_msg.shape[0]
    saved = []
    for layer_index in range(layer_total):
        if layer_index == 0:
            first_rows = jnp.dot(ext_onehot, first_table, precision=exact_mode)
            lent_ext = first_rows[None]
        else:
            lent_own = jnp.einsum("bac,cd->bad", hidden, w_msg[layer_index], precision=exact_mode)
            outgoing_rows = jnp.einsum("ga,bac->bgc", selector, lent_own, precision=exact_mode)
            arrived_rows = with_halo(outgoing_rows, (("space", 1),), ghost_count)
            lent_ext = jnp.concatenate(
                [lent_own, arrived_rows[:, :ghost_count], arrived_rows[:, 3 * ghost_count :]],
                axis=1,
            )
        radial_map = w_radial[layer_index]
        per_block = lax.map(
            lambda parts: block_message(
                lent_ext, parts[0], parts[1], parts[2], radial_map, edge_scale
            ),
            (blocks_basis, blocks_live, blocks_rows),
        )
        message = unblocked(per_block, 1)
        update = jnp.einsum("bac,cd->bad", message, w_upd[layer_index], precision=exact_mode)
        saved.append((lent_ext, update))
        hidden = hidden + jax.nn.silu(update)
    grad_hidden = jnp.broadcast_to(w_out[None, None], hidden.shape)
    grad_points = jnp.zeros(ext_points.shape, jnp.float32)
    center_pull = jnp.zeros(reduced.shape, jnp.float32)
    for layer_index in reversed(range(layer_total)):
        lent_ext, update = saved[layer_index]
        grad_update = grad_hidden * silu_slope(update)
        grad_message = jnp.einsum(
            "bac,dc->bad", grad_update, w_upd[layer_index], precision=exact_mode
        )
        want_features = layer_index > 0
        if want_features:
            start_lent = jnp.zeros(lent_ext.shape, jnp.float32)
        else:
            start_lent = jnp.zeros((1,), jnp.float32)
        step_function = partial(
            block_backward,
            lent_ext=lent_ext,
            radial_map=w_radial[layer_index],
            edge_scale=edge_scale,
            want_features=want_features,
        )
        scanned = (
            blocks_basis,
            blocks_offsets,
            blocks_displace,
            blocks_distance,
            blocks_live,
            blocks_rows,
            blocked(grad_message, 1),
        )
        (grad_lent, grad_points), pulls = lax.scan(
            step_function, (start_lent, grad_points), scanned
        )
        center_pull = center_pull + unblocked(pulls, 2)
        if want_features:
            sent_back = with_halo(grad_lent[:, atom_count:], (("space", 1),), ghost_count)
            returned = jnp.concatenate(
                [sent_back[:, :ghost_count], sent_back[:, 3 * ghost_count :]], axis=1
            )
            grad_own = grad_lent[:, :atom_count] + jnp.einsum(
                "ga,bgc->bac", selector, returned, precision=exact_mode
            )
            grad_hidden = grad_hidden + jnp.einsum(
                "bac,dc->bad", grad_own, w_msg[layer_index], precision=exact_mode
            )
    sent_force = with_halo(grad_points[:, :, atom_count:], (("space", 2),), ghost_count)
    returned_force = jnp.concatenate(
        [sent_force[:, :, :ghost_count], sent_force[:, :, 3 * ghost_count :]], axis=2
    )
    energy_grad = (
        grad_points[:, :, :atom_count]
        + center_pull
        + jnp.einsum("ga,bcg->bca", selector, returned_force, precision=exact_mode)
    )
    pull_reduced = -energy_grad
    ratio = float(beads_all) / PC
    weights = own_columns
    return ratio * jnp.einsum(
        "kj,kcn->jcn",
        weights,
        lax.all_gather(pull_reduced, "bead", axis=0, tiled=True),
        precision=exact_mode,
    )


def solution(mesh):
    return jax.shard_map(
        on_device,
        mesh=mesh,
        in_specs=(
            P("bead", None, "space"),
            P("space"),
            P(None, "space"),
            P("space"),
            P("space"),
            P(),
            P(),
            P(),
            P(),
            P(),
        ),
        out_specs=P("bead", None, "space"),
        check_vma=False,
    )
```

profile of v0, /device:TPU:64, one launch (start us, length us, event | category | flops | bytes accessed | tf_op | source)
XLA Modules:
  0.0 223.0 jit_solution(11656162681923624815)
XLA Ops:
  0.7 42.8 %all_gather.6 = f32[64,3,256]{2,1,0:T(4,128)S(1)} all-gather(f32[4,3,256]{2,1,0:T(4,128)S(1)} %copy.41), channel_id=1, replica_groups=mesh['bead'=16,'space'=16] {'bead'}, dimensions={0}, use_global_device_ids=true | all-gather | bytes 208896 | tf_op jit(solution)/shard_map/all_gather | solution.py:115
  46.7 3.8 %collective-permute-start.1 = (f32[1,4,64]{2,1,0:T(4,128)S(1)}, f32[1,4,64]{2,1,0:T(4,128)S(1)}, u32[]{:S(2)}, u32[]{:S(2)}) collective-permute-start(f32[1,4,64]{2,1,0:T(4,128)S(1)} %get-tuple-element.553), channel_id=1, source_target_pairs={{1,0},{2,1},{3,2},{4,3},{5,4},{6,5},{7,6},{8,7},{9,8},{10,9},{11,1... | collective-permute-start | bytes 3080 | tf_op jit(solution)/shard_map/ppermute | solution.py:27
  55.1 7.0 %while.58 = (s32[]{:T(128)}, f32[2,1,3,32,128]{4,2,3,1,0:T(4,128)S(1)}, s32[2,32,128]{2,1,0:T(8,128)S(1)}, f32[1,3,384]{2,1,0:T(4,128)S(1)}, s32[]{:T(128)}) while((s32[]{:T(128)}, f32[2,1,3,32,128]{4,2,3,1,0:T(4,128)S(1)}, s32[2,32,128]{2,1,0:T(8,128)S(1)}, f32[1,3,384]{2,1,0:T(4,128)S(1)}, s32[]{:T(128)}) %tuple.106), condition=%wide.region_1.2_spmd, body=%wide.region_0.1_spmd.sunk | while | flops 58195968 | bytes 120901 | solution.py:144
  55.2 3.5 %fusion.252 = f32[2,1,3,32,128]{4,2,3,1,0:T(4,128)S(1)} fusion(f32[2,1,3,32,128]{4,2,3,1,0:T(4,128)S(1)} %get-tuple-element.823, s32[]{:T(128)} %get-tuple-element.822, s32[32,128]{1,0:T(8,128)S(1)} %dynamic-slice_bitcast_fusion.22, f32[1,3,384]{2,1,0:T(4,128)S(1)} %get-tuple-element.830), kind=kOutput, calls=%fused_computation.4.clone.1 | convolution fusion | flops 58195968 | bytes 88068 | tf_op jit(solution)/shard_map/while/body/eval_jaxpr/kre,bce->bckr/dot_general | solution.py:142
  58.7 3.5 %fusion.252 = f32[2,1,3,32,128]{4,2,3,1,0:T(4,128)S(1)} fusion(f32[2,1,3,32,128]{4,2,3,1,0:T(4,128)S(1)} %get-tuple-element.823, s32[]{:T(128)} %get-tuple-element.822, s32[32,128]{1,0:T(8,128)S(1)} %dynamic-slice_bitcast_fusion.22, f32[1,3,384]{2,1,0:T(4,128)S(1)} %get-tuple-element.830), kind=kOutput, calls=%fused_computation.4.clone.1 | convolution fusion | flops 58195968 | bytes 88068 | tf_op jit(solution)/shard_map/while/body/eval_jaxpr/kre,bce->bckr/dot_general | solution.py:142
  62.9 19.7 %while.59 = (s32[]{:T(128)}, f32[2,1,128,128]{3,2,1,0:T(8,128)S(1)}, f32[2,32,128]{2,1,0:T(8,128)S(1)}, f32[2,8,1,32,128]{4,1,3,2,0:T(8,128)S(1)}, f32[8,128]{1,...) while((s32[]{:T(128)}, f32[2,1,128,128]{3,2,1,0:T(8,128)S(1)}, ...), condition=%wide.region_4.5_spmd, body=%wide.region_3.4_spmd.sunk | while | flops 2474655744 | bytes 9048165 | solution.py:182
  62.9 3.4 %fusion.258 = f32[32,128,128]{2,1,0:T(8,128)S(1)} fusion(f32[2,8,1,32,128]{4,1,3,2,0:T(8,128)S(1)} %get-tuple-element.851, s32[]{:T(128)} %get-tuple-element.840, f32[8,128]{1,0:T(8,128)S(1)} %get-tuple-element.852), kind=kOutput, calls=%fused_computation.15.clone.1 | convolution fusion | flops 50331648 | bytes 2232324 | tf_op jit(solution)/shard_map/while/body/eval_jaxpr/nbkr,nc->bkrc/dot_general | solution.py:70
  66.4 3.3 %fusion.259 = f32[32,128,128]{2,1,0:T(8,128)S(1)} fusion(f32[32,128,128]{2,1,0:T(8,128)S(1)} %fusion.258, s32[32,128]{1,0:T(8,128)S(1)} %dynamic-slice_bitcast_fusion.24, f32[1,384,128]{2,1,0:T(8,128)S(1)} %get-tuple-element.854), kind=kOutput, calls=%fused_computation.11.clone.1 | convolution fusion | flops 2418016256 | bytes 4407296 | tf_op jit(solution)/shard_map/while/body/eval_jaxpr/kre,bec->bkrc/dot_general | solution.py:72
  72.8 3.4 %fusion.258 = f32[32,128,128]{2,1,0:T(8,128)S(1)} fusion(f32[2,8,1,32,128]{4,1,3,2,0:T(8,128)S(1)} %get-tuple-element.851, s32[]{:T(128)} %get-tuple-element.840, f32[8,128]{1,0:T(8,128)S(1)} %get-tuple-element.852), kind=kOutput, calls=%fused_computation.15.clone.1 | convolution fusion | flops 50331648 | bytes 2232324 | tf_op jit(solution)/shard_map/while/body/eval_jaxpr/nbkr,nc->bkrc/dot_general | solution.py:70
  76.2 3.3 %fusion.259 = f32[32,128,128]{2,1,0:T(8,128)S(1)} fusion(f32[32,128,128]{2,1,0:T(8,128)S(1)} %fusion.258, s32[32,128]{1,0:T(8,128)S(1)} %dynamic-slice_bitcast_fusion.24, f32[1,384,128]{2,1,0:T(8,128)S(1)} %get-tuple-element.854), kind=kOutput, calls=%fused_computation.11.clone.1 | convolution fusion | flops 2418016256 | bytes 4407296 | tf_op jit(solution)/shard_map/while/body/eval_jaxpr/kre,bec->bkrc/dot_general | solution.py:72
  85.3 4.0 %collective-permute-start.3 = (f32[1,64,128]{2,1,0:T(8,128)S(1)}, f32[1,64,128]{2,1,0:T(8,128)S(1)}, u32[]{:S(2)}, u32[]{:S(2)}) collective-permute-start(f32[1,64,128]{2,1,0:T(8,128)S(1)} %get-tuple-element.538), channel_id=1, source_target_pairs={{1,0},{2,1},{3,2},{4,3},{5,4},{6,5},{7,6},{8,7},{9,8},{10,9},{11,1... | collective-permute-start | bytes 98312 | tf_op jit(solution)/shard_map/ppermute | solution.py:27
  91.6 20.9 %while.60 = (s32[]{:T(128)}, f32[2,1,128,128]{3,2,1,0:T(8,128)}, f32[2,32,128]{2,1,0:T(8,128)S(1)}, f32[2,8,1,32,128]{4,1,3,2,0:T(8,128)S(1)}, f32[8,128]{1,0:T(...) while((s32[]{:T(128)}, f32[2,1,128,128]{3,2,1,0:T(8,128)}, ...), condition=%wide.region_6.7_spmd, body=%wide.region_5.6_spmd.sunk | while | flops 2474655744 | bytes 9048673 | solution.py:182
  91.6 3.4 %fusion.266 = f32[32,128,128]{2,1,0:T(8,128)S(1)} fusion(f32[2,8,1,32,128]{4,1,3,2,0:T(8,128)S(1)} %get-tuple-element.875, s32[]{:T(128)} %get-tuple-element.864, f32[8,128]{1,0:T(8,128)S(1)} %get-tuple-element.876), kind=kOutput, calls=%fused_computation.31.clone.1 | convolution fusion | flops 50331648 | bytes 2232324 | tf_op jit(solution)/shard_map/while/body/eval_jaxpr/nbkr,nc->bkrc/dot_general | solution.py:70
  95.1 3.3 %fusion.267 = f32[32,128,128]{2,1,0:T(8,128)S(1)} fusion(f32[32,128,128]{2,1,0:T(8,128)S(1)} %fusion.266, s32[32,128]{1,0:T(8,128)S(1)} %dynamic-slice_bitcast_fusion.26, f32[1,384,128]{2,1,0:T(8,128)S(1)} %get-tuple-element.878), kind=kOutput, calls=%fused_computation.27.clone.1 | convolution fusion | flops 2418016256 | bytes 4407296 | tf_op jit(solution)/shard_map/while/body/eval_jaxpr/kre,bec->bkrc/dot_general | solution.py:72
  102.1 3.4 %fusion.266 = f32[32,128,128]{2,1,0:T(8,128)S(1)} fusion(f32[2,8,1,32,128]{4,1,3,2,0:T(8,128)S(1)} %get-tuple-element.875, s32[]{:T(128)} %get-tuple-element.864, f32[8,128]{1,0:T(8,128)S(1)} %get-tuple-element.876), kind=kOutput, calls=%fused_computation.31.clone.1 | convolution fusion | flops 50331648 | bytes 2232324 | tf_op jit(solution)/shard_map/while/body/eval_jaxpr/nbkr,nc->bkrc/dot_general | solution.py:70
  114.0 32.4 %while.62 = (s32[]{:T(128)}, f32[1,384,128]{1,2,0:T(8,128)}, f32[1,3,384]{2,1,0:T(4,128)S(1)}, f32[2,1,3,128]{3,2,1,0:T(4,128)S(1)}, f32[2,32,128]{2,1,0:T(8,128...) while((s32[]{:T(128)}, f32[1,384,128]{1,2,0:T(8,128)}, ...), condition=%wide.region_10.11_spmd.clone, body=%wide.region_7.10_spmd.clone.sunk | while | flops 4996204544 | bytes 10068156 | solution.py:222
  114.2 3.4 %fusion.284 = f32[32,128,128]{2,1,0:T(8,128)S(1)} fusion(f32[2,8,1,32,128]{4,1,3,2,0:T(8,128)S(1)} %get-tuple-element.916, s32[]{:T(128)} %get-tuple-element.895, f32[8,128]{1,0:T(8,128)S(1)} %get-tuple-element.917), kind=kOutput, calls=%fused_computation.99.clone.1 | convolution fusion | flops 50331648 | bytes 2232324 | tf_op jit(solution)/shard_map/while/body/eval_jaxpr/nbkr,nc->bkrc/dot_general | solution.py:81
  117.8 4.2 %fusion.285 = f32[1,384,128]{1,2,0:T(8,128)} fusion(s32[32,128]{1,0:T(8,128)S(1)} %dynamic-slice_bitcast_fusion.30, f32[32,128,128]{2,1,0:T(8,128)S(1)} %fusion.284, f32[128,128]{1,0:T(8,128)S(1)} %dynamic-slice_bitcast_fusion.31, f32[32,128]{1,0:T(8,128)S(1)} %multiply_bitcast_fusion.5, f32[1,384,128]{1,2,0:T(8,128)} %get-tuple-element.896, ...), kind=kOutput, calls=%fused_computation.87.clone.1 | convolution fusion | flops 2418638848 | bytes 2588673 | tf_op jit(solution)/shard_map/while/body/eval_jaxpr/kre,bkrc->bec/dot_general | solution.py:94
  129.9 3.4 %fusion.284 = f32[32,128,128]{2,1,0:T(8,128)S(1)} fusion(f32[2,8,1,32,128]{4,1,3,2,0:T(8,128)S(1)} %get-tuple-element.916, s32[]{:T(128)} %get-tuple-element.895, f32[8,128]{1,0:T(8,128)S(1)} %get-tuple-element.917), kind=kOutput, calls=%fused_computation.99.clone.1 | convolution fusion | flops 50331648 | bytes 2232324 | tf_op jit(solution)/shard_map/while/body/eval_jaxpr/nbkr,nc->bkrc/dot_general | solution.py:81
  133.4 5.1 %fusion.285 = f32[1,384,128]{1,2,0:T(8,128)} fusion(s32[32,128]{1,0:T(8,128)S(1)} %dynamic-slice_bitcast_fusion.30, f32[32,128,128]{2,1,0:T(8,128)S(1)} %fusion.284, f32[128,128]{1,0:T(8,128)S(1)} %dynamic-slice_bitcast_fusion.31, f32[32,128]{1,0:T(8,128)S(1)} %multiply_bitcast_fusion.5, f32[1,384,128]{1,2,0:T(8,128)} %get-tuple-element.896, ...), kind=kOutput, calls=%fused_computation.87.clone.1 | convolution fusion | flops 2418638848 | bytes 2588673 | tf_op jit(solution)/shard_map/while/body/eval_jaxpr/kre,bkrc->bec/dot_general | solution.py:94
  147.8 3.9 %collective-permute-start.5 = (f32[1,64,128]{1,2,0:T(8,128)S(1)}, f32[1,64,128]{1,2,0:T(8,128)S(1)}, u32[]{:S(2)}, u32[]{:S(2)}) collective-permute-start(f32[1,64,128]{1,2,0:T(8,128)S(1)} %get-tuple-element.536), channel_id=1, source_target_pairs={{1,0},{2,1},{3,2},{4,3},{5,4},{6,5},{7,6},{8,7},{9,8},{10,9},{11,1... | collective-permute-start | bytes 98312 | tf_op jit(solution)/shard_map/ppermute | solution.py:27
  157.3 16.0 %while.61 = (s32[]{:T(128)}, f32[1,3,384]{2,1,0:T(4,128)S(1)}, f32[2,1,3,128]{3,2,1,0:T(4,128)S(1)}, f32[2,32,128]{2,1,0:T(8,128)S(1)}, f32[2,1,128,128]{3,2,1,0...) while((s32[]{:T(128)}, f32[1,3,384]{2,1,0:T(4,128)S(1)}, ...), condition=%wide.region_14.15_spmd, body=%wide.region_11.14_spmd.sunk | while | flops 2527233024 | bytes 5247133 | solution.py:222
  173.3 4.0 %collective-permute-start.7 = (f32[1,3,64]{2,1,0:T(4,128)S(1)}, f32[1,3,64]{2,1,0:T(4,128)S(1)}, u32[]{:S(2)}, u32[]{:S(2)}) collective-permute-start(f32[1,3,64]{2,1,0:T(4,128)S(1)} %get-tuple-element.546), channel_id=1, source_target_pairs={{1,0},{2,1},{3,2},{4,3},{5,4},{6,5},{7,6},{8,7},{9,8},{10,9},{11,1... | collective-permute-start | bytes 2312 | tf_op jit(solution)/shard_map/ppermute | solution.py:27
  178.8 43.0 %all_gather.7 = f32[16,3,256]{2,1,0:T(4,128)S(1)} all-gather(f32[1,3,256]{2,1,0:T(4,128)S(1)} %fusion.116), channel_id=1, replica_groups=mesh['bead'=16,'space'=16] {'bead'}, dimensions={0}, use_global_device_ids=true | all-gather | bytes 52224 | tf_op jit(solution)/shard_map/all_gather | solution.py:252
  (138 shorter events, 73.3 us)
Async XLA Ops:
  0.0 52.6 %copy-start = (f32[2,128]{1,0:T(2,128)S(1)}, f32[2,128]{1,0:T(2,128)}, u32[]{:S(2)}) copy-start(f32[2,128]{1,0:T(2,128)} %param.27) | copy-start | bytes 3076
  46.7 7.8 %collective-permute-start = (f32[1,4,64]{2,1,0:T(4,128)S(1)}, f32[1,4,64]{2,1,0:T(4,128)S(1)}, u32[]{:S(2)}, u32[]{:S(2)}) collective-permute-start(f32[1,4,64]{2,1,0:T(4,128)S(1)} %get-tuple-element.552), channel_id=1, source_target_pairs={{0,1},{1,2},{2,3},{3,4},{4,5},{5,6},{6,7},{7,8},{8,9},{9,10},{10,1... | collective-permute-start | bytes 3080 | tf_op jit(solution)/shard_map/ppermute | solution.py:24
  46.7 7.8 %collective-permute-start.1 = (f32[1,4,64]{2,1,0:T(4,128)S(1)}, f32[1,4,64]{2,1,0:T(4,128)S(1)}, u32[]{:S(2)}, u32[]{:S(2)}) collective-permute-start(f32[1,4,64]{2,1,0:T(4,128)S(1)} %get-tuple-element.553), channel_id=1, source_target_pairs={{1,0},{2,1},{3,2},{4,3},{5,4},{6,5},{7,6},{8,7},{9,8},{10,9},{11,1... | collective-permute-start | bytes 3080 | tf_op jit(solution)/shard_map/ppermute | solution.py:27
  62.9 19.7 %copy-start.1 = (f32[2,128,128]{2,1,0:T(8,128)S(1)}, f32[2,128,128]{2,1,0:T(8,128)}, u32[]{:S(2)}) copy-start(f32[2,128,128]{2,1,0:T(8,128)} %param.30) | copy-start | bytes 393220
  62.9 20.7 %copy-start.3 = (s32[256]{0:T(256)S(1)}, s32[256]{0:T(256)}, u32[]{:S(2)}) copy-start(s32[256]{0:T(256)} %param.23) | copy-start | bytes 3076
  62.9 22.1 %copy-start.4 = (s32[128]{0:T(128)S(1)}, s32[128]{0:T(128)}, u32[]{:S(2)}) copy-start(s32[128]{0:T(128)} %param.26) | copy-start | bytes 1540
  82.9 0.6 copy-start.2
  85.2 5.5 %collective-permute-start.2 = (f32[1,64,128]{2,1,0:T(8,128)S(1)}, f32[1,64,128]{2,1,0:T(8,128)S(1)}, u32[]{:S(2)}, u32[]{:S(2)}) collective-permute-start(f32[1,64,128]{2,1,0:T(8,128)S(1)} %get-tuple-element.537), channel_id=1, source_target_pairs={{0,1},{1,2},{2,3},{3,4},{4,5},{5,6},{6,7},{7,8},{8,9},{9,10},{10,1... | collective-permute-start | bytes 98312 | tf_op jit(solution)/shard_map/ppermute | solution.py:24
  85.3 5.6 %collective-permute-start.3 = (f32[1,64,128]{2,1,0:T(8,128)S(1)}, f32[1,64,128]{2,1,0:T(8,128)S(1)}, u32[]{:S(2)}, u32[]{:S(2)}) collective-permute-start(f32[1,64,128]{2,1,0:T(8,128)S(1)} %get-tuple-element.538), channel_id=1, source_target_pairs={{1,0},{2,1},{3,2},{4,3},{5,4},{6,5},{7,6},{8,7},{9,8},{10,9},{11,1... | collective-permute-start | bytes 98312 | tf_op jit(solution)/shard_map/ppermute | solution.py:27
  91.6 20.9 %copy-start.5 = (f32[128]{0:T(128)S(1)}, f32[128]{0:T(128)}, u32[]{:S(2)}) copy-start(f32[128]{0:T(128)} %param.31) | copy-start | bytes 1540
  147.4 6.1 %collective-permute-start.4 = (f32[1,64,128]{1,2,0:T(8,128)S(1)}, f32[1,64,128]{1,2,0:T(8,128)S(1)}, u32[]{:S(2)}, u32[]{:S(2)}) collective-permute-start(f32[1,64,128]{1,2,0:T(8,128)S(1)} %get-tuple-element.535), channel_id=1, source_target_pairs={{0,1},{1,2},{2,3},{3,4},{4,5},{5,6},{6,7},{7,8},{8,9},{9,10},{10,1... | collective-permute-start | bytes 98312 | tf_op jit(solution)/shard_map/ppermute | solution.py:24
  147.8 5.8 %collective-permute-start.5 = (f32[1,64,128]{1,2,0:T(8,128)S(1)}, f32[1,64,128]{1,2,0:T(8,128)S(1)}, u32[]{:S(2)}, u32[]{:S(2)}) collective-permute-start(f32[1,64,128]{1,2,0:T(8,128)S(1)} %get-tuple-element.536), channel_id=1, source_target_pairs={{1,0},{2,1},{3,2},{4,3},{5,4},{6,5},{7,6},{8,7},{9,8},{10,9},{11,1... | collective-permute-start | bytes 98312 | tf_op jit(solution)/shard_map/ppermute | solution.py:27
  173.3 5.2 %collective-permute-start.6 = (f32[1,3,64]{2,1,0:T(4,128)S(1)}, f32[1,3,64]{2,1,0:T(4,128)S(1)}, u32[]{:S(2)}, u32[]{:S(2)}) collective-permute-start(f32[1,3,64]{2,1,0:T(4,128)S(1)} %get-tuple-element.545), channel_id=1, source_target_pairs={{0,1},{1,2},{2,3},{3,4},{4,5},{5,6},{6,7},{7,8},{8,9},{9,10},{10,1... | collective-permute-start | bytes 2312 | tf_op jit(solution)/shard_map/ppermute | solution.py:24
  173.3 5.3 %collective-permute-start.7 = (f32[1,3,64]{2,1,0:T(4,128)S(1)}, f32[1,3,64]{2,1,0:T(4,128)S(1)}, u32[]{:S(2)}, u32[]{:S(2)}) collective-permute-start(f32[1,3,64]{2,1,0:T(4,128)S(1)} %get-tuple-element.546), channel_id=1, source_target_pairs={{1,0},{2,1},{3,2},{4,3},{5,4},{6,5},{7,6},{8,7},{9,8},{10,9},{11,1... | collective-permute-start | bytes 2312 | tf_op jit(solution)/shard_map/ppermute | solution.py:27
where the time goes:
time: 226 us; the launch traced here: 223 us
  matrix products  104 us (46%)
  blocking collectives  85.8 us (38%)
  starting transfers between devices  16.2 us (7%)
  local copies, waits for them, and re-layouts  5.85 us (3%)
  waiting for transfers between devices  4.79 us (2%)
  other arithmetic  4.56 us (2%)
    all_gather x1, blocking collectives, on_device(): lax.all_gather(pull_reduced, 'bead', axis=0, tiled=True)  43 us
    all_gather x1, blocking collectives, on_device(): lax.all_gather(positions, 'bead', axis=0, tiled=True)  42.8 us
    ppermute x4, starting transfers between devices, with_halo(): lax.ppermute(lax.slice_in_dim(block, 0, width, axis=dim), axis, backward)  15.7 us
    dot_general x4, matrix products, block_message(): jnp.einsum('nbkr,nc->bkrc', radial_basis, radial_map, precision=exact_mode)  13.8 us
    dot_general x4, matrix products, block_message(): jnp.einsum('kre,bec->bkrc', chooser, lent_ext, precision=exact_mode)  13.3 us
    dot_general x4, matrix products, block_backward(): jnp.einsum('kre,bec->bkrc', chooser, lent_ext, precision=exact_mode)  13 us
    dot_general x4, matrix products, block_message(): jnp.einsum('bkrc,kr->brc', radial_w * near_rows, live_slots, precision=ex...  11.6 us
    dot_general x4, matrix products, block_backward(): jnp.einsum('bkrc,nc->nbkr', grad_radial, radial_map, precision=exact_mode)  9.4 us
  transfers between devices with their start and end apart: 8, of which 5 were waited for; matrix products, arithmetic and copies ran while one was open for 2% of the time, Pallas kernels for 0%

commit v1 on v0

v1 whole, which is shorter than its diff:
```python
import functools
import math

import jax
import jax.numpy as jnp
from jax import lax
from jax.experimental import pallas as pl
from jax.experimental.pallas import tpu as pltpu
from jax.sharding import PartitionSpec as P

MESH = pl.DeviceIdType.MESH
HI = lax.Precision.HIGHEST
F32 = jnp.float32
BF16 = jnp.bfloat16

NB = 8
CH = 128
A = 256
G = 64
E = A + 2 * G
K = 32
H = 128
ROOT = math.sqrt(math.log2(math.e))
STEP = ROOT / 0.2
CENTERS = tuple(STEP * 1.5 * b / (NB - 1) for b in range(NB))
FLOOR = 0.01


def table_value(lag, beads, reduced):
    t = lag / beads
    total = 1.0 + math.cos(math.pi * reduced * t)
    for m in range(1, reduced // 2):
        total += 2.0 * math.cos(2.0 * math.pi * m * t)
    return total / beads


def split(v):
    hi = v.astype(BF16)
    lo = (v - hi.astype(F32)).astype(BF16)
    return hi, lo


def exact_dot(a, b):
    return jnp.dot(a, b, precision=HI, preferred_element_type=F32)


def exact_dot_nt(a, b):
    return lax.dot_general(
        a, b, (((1,), (1,)), ((), ())), precision=HI, preferred_element_type=F32
    )


def fast_dot(a, b):
    return jnp.dot(a, b, preferred_element_type=F32)


def kernel(
    nb, ns, own,
    pos_h, spc_h, nbr_h, cnt_h, snd_h, emb_h, wr_h, wm_h, wu_h, wo_h,
    out_ref,
    pos_v, spc_v, nbr_v, cnt_v, snd_v, emb_v, wr_v, wm_v, wu_v, wo_v,
    tx1, rx1, spc_l, spc_r, snd_l, snd_r, red_v, red_l, red_r,
    idx_v, cnt_mat, gcol, cen, w1bc, wu1t, wocol, p0, p0r, h0_v, slope0,
    ah_own, al_own, ah_gh, al_gh, z_v, rinv_v, l_v, x_v, xg_v, q_v, dl_own, dl_gh, r4_v,
    fold_v, tx5, r5_l, r5_r, tx6, rx6,
    load_sem, s1, r1, sa, ra, s2, r2, s3, r3, s4, r4, s5, r5, s6, r6,
):
    beads, reduced = nb * own, nb
    scale = K ** -0.5
    b = lax.axis_index("bead")
    d = lax.axis_index("space")
    left = lax.rem(d + (ns - 1), ns)
    right = lax.rem(d + 1, ns)
    peers = [lax.rem(b + lag, nb) for lag in range(nb)]

    def bead_copy(src, dst, ss, rs, lag):
        return pltpu.make_async_remote_copy(
            src_ref=src, dst_ref=dst, send_sem=ss, recv_sem=rs,
            device_id={"bead": peers[lag]}, device_id_type=MESH)

    def side_copy(src, dst, ss, rs, side):
        return pltpu.make_async_remote_copy(
            src_ref=src, dst_ref=dst, send_sem=ss, recv_sem=rs,
            device_id={"space": side}, device_id_type=MESH)

    barrier = pltpu.get_barrier_semaphore()
    for lag in range(1, nb):
        pl.semaphore_signal(barrier, inc=1, device_id={"bead": peers[lag]}, device_id_type=MESH)
    for side in (left, right):
        pl.semaphore_signal(barrier, inc=1, device_id={"space": side}, device_id_type=MESH)

    loads = []
    for i, (src, dst) in enumerate((
        (pos_h, pos_v), (spc_h, spc_v), (snd_h, snd_v), (nbr_h, nbr_v), (cnt_h, cnt_v),
        (emb_h, emb_v), (wr_h, wr_v), (wm_h, wm_v), (wu_h, wu_v), (wo_h, wo_v),
    )):
        copy = pltpu.make_async_copy(src, dst, load_sem.at[i])
        copy.start()
        loads.append(copy)

    loads[0].wait()
    packed = []
    for j in range(own):
        packed.append(jnp.concatenate(
            [pos_v[c, j : j + 1, half * H : half * H + H] for half in range(2) for c in range(3)], axis=0))
    for lag in range(nb):
        total = None
        for j in range(own):
            term = table_value(own * lag - j, beads, reduced) * packed[j]
            total = term if total is None else total + term
        tx1[lag] = total
    loads[1].wait()
    loads[2].wait()
    pl.semaphore_wait(barrier, nb + 1)

    first = [None] + [
        bead_copy(tx1.at[lag], rx1.at[lag], s1.at[lag], r1.at[lag], lag) for lag in range(1, nb)
    ]
    for lag in range(1, nb):
        first[lag].start()
    aux = [
        side_copy(spc_v, spc_r, sa.at[0], ra.at[0], left),
        side_copy(spc_v, spc_l, sa.at[1], ra.at[1], right),
        side_copy(snd_v, snd_r, sa.at[2], ra.at[2], left),
        side_copy(snd_v, snd_l, sa.at[3], ra.at[3], right),
    ]
    for copy in aux:
        copy.start()

    for copy in loads[3:]:
        copy.wait()
    n = nbr_v[...]
    n = jnp.where(n >= A + G, n - G, jnp.where(n >= A, n + G, n))
    slot = lax.broadcasted_iota(jnp.int32, (K, A), 0)
    idx_v[...] = jnp.where(slot < cnt_v[...], n, -1)

    def count_rows(i, carry):
        base = pl.multiple_of(i * 32, 32)
        row = lax.broadcasted_iota(jnp.int32, (32, A), 0) + base
        acc = jnp.zeros((32, A), F32)
        for k in range(K):
            acc = acc + jnp.where(idx_v[k : k + 1, :] == row, 1.0, 0.0)
        cnt_mat[pl.ds(base, 32), :] = acc
        return carry

    lax.fori_loop(0, E // 32, count_rows, 0)

    zeros6 = jnp.zeros((6, CH), F32)
    emb8 = jnp.concatenate([emb_v[...], zeros6], axis=0)
    table = exact_dot(emb8, wm_v[0])
    w0 = wr_v[0] * scale
    rows0 = jnp.concatenate([w0 * table[0:1], w0 * (table[1:2] - table[0:1])], axis=0)
    p0_now = exact_dot(rows0, wu_v[0])
    p0[...] = p0_now
    for j in range(2 * NB):
        p0r[pl.ds(8 * j, 8), :] = jnp.broadcast_to(p0_now[j : j + 1, :], (8, CH))
    w1 = wr_v[1] * scale
    w1t = jnp.transpose(jnp.concatenate([w1, jnp.zeros((CH - NB, CH), F32)], axis=0))
    for k in range(NB):
        w1bc[k] = jnp.broadcast_to(w1t[:, k : k + 1], (CH, H))
    wu1t[...] = jnp.transpose(wu_v[1])
    wot = jnp.transpose(jnp.broadcast_to(wo_v[...], (CH, CH)))
    wocol[...] = wot

    for copy in aux:
        copy.wait_recv()
    lane = lax.broadcasted_iota(jnp.int32, (1, H), 1)
    low = lane < G
    order = jnp.where(low, snd_r[...], snd_l[...] - (A - H))
    turn = jnp.where(
        lax.broadcasted_iota(jnp.int32, (H, H), 0) == order, 1.0, 0.0
    ).astype(BF16)
    cnt_mat[pl.ds(A, 2 * G), :] = fast_dot(turn, cnt_mat[pl.ds(A, 2 * G), :].astype(BF16))
    kind_own = spc_v[...].astype(F32)
    kind_gh = jnp.where(low, spc_r[0:1, :], spc_l[1:2, :]).astype(F32)
    zrest = jnp.zeros((CH - 4, H), F32)
    z3 = jnp.zeros((3, H), F32)
    for half in range(2):
        kcol = jnp.transpose(jnp.concatenate([z3, kind_own[half : half + 1], zrest], axis=0))
        h0_v[pl.ds(half * H, H), :] = jnp.where(
            kcol[:, 3:4] > 0.5, emb_v[1:2, :], emb_v[0:1, :])

    red = tx1[0]
    for lag in range(1, nb):
        first[lag].wait_recv()
        red = red + rx1[lag]
    red_v[...] = red
    second = [
        side_copy(red_v, red_r, s2.at[0], r2.at[0], left),
        side_copy(red_v, red_l, s2.at[1], r2.at[1], right),
    ]
    for copy in second:
        copy.start()
    cen[...] = jnp.concatenate(
        [jnp.concatenate([red[0:3], red[3:6]], axis=1), jnp.zeros((5, A), F32)], axis=0)
    for half in range(2):
        gcol[pl.ds(half * H, H), :] = jnp.transpose(jnp.concatenate(
            [red[3 * half : 3 * half + 3], kind_own[half : half + 1], zrest], axis=0))

    def pair_rows(start, ah, al, local):
        rows = 16

        def step(i, carry):
            base = pl.multiple_of(start + i * rows, rows)
            put = pl.multiple_of(i * rows, rows)
            col = gcol[pl.ds(base, rows), :]
            dx = col[:, 0:1] - cen[0:1, :]
            dy = col[:, 1:2] - cen[1:2, :]
            dz = col[:, 2:3] - cen[2:3, :]
            kind = jnp.broadcast_to(col[:, 3:4], (rows, A))
            square = dx * dx + dy * dy + dz * dz + FLOOR
            rinv = lax.rsqrt(square)
            x = square * rinv * STEP
            rinv_v[pl.ds(base, rows), :] = rinv
            c = cnt_mat[pl.ds(base, rows), :]
            sums = list(carry)
            for k in range(NB):
                off = x - CENTERS[k]
                a = c * jnp.exp2(-(off * off))
                hi, lo = split(a)
                ah[pl.ds(k * local + put, rows), :] = hi
                al[pl.ds(k * local + put, rows), :] = lo
                z_v[pl.ds(k * E + base, rows), :] = a * off
                s = a * kind
                sums[k] = sums[k] + (a[0:8] + a[8:16])
                sums[NB + k] = sums[NB + k] + (s[0:8] + s[8:16])
            return tuple(sums)

        return step

    sums = tuple(jnp.zeros((8, A), F32) for _ in range(2 * NB))
    sums = lax.fori_loop(0, A // 16, pair_rows(0, ah_own, al_own, A), sums)
    for copy in second:
        copy.wait_recv()
    ghost = jnp.where(low, red_r[0:3, :], red_l[3:6, :])
    shift_right = jnp.where(d == ns - 1, float(ns), 0.0)
    shift_left = jnp.where(d == 0, -float(ns), 0.0)
    shift = jnp.where(low, shift_right, shift_left)
    first_row = lax.broadcasted_iota(jnp.int32, (3, H), 0) == 0
    ghost = ghost + jnp.where(first_row, shift, 0.0)
    gcol[pl.ds(A, H), :] = jnp.transpose(jnp.concatenate([ghost, kind_gh, zrest], axis=0))
    sums = lax.fori_loop(0, 2 * G // 16, pair_rows(A, ah_gh, al_gh, 2 * G), sums)

    stacked = jnp.concatenate(sums, axis=0)
    u0 = exact_dot(jnp.transpose(stacked), p0r[...])
    sig0 = 1.0 / (1.0 + jnp.exp(-u0))
    slope0[...] = sig0 * (1.0 + u0 * (1.0 - sig0))
    h1 = h0_v[...] + u0 * sig0
    lent = exact_dot(h1, wm_v[1])
    l_v[pl.ds(0, A), :] = lent
    third = [
        side_copy(l_v.at[pl.ds(0, G)], l_v.at[pl.ds(A, G)], s3.at[0], r3.at[0], left),
        side_copy(l_v.at[pl.ds(A - G, G)], l_v.at[pl.ds(A + G, G)], s3.at[1], r3.at[1], right),
    ]
    for copy in third:
        copy.start()

    lt = jnp.transpose(lent)
    for k in range(NB):
        w = w1bc[k]
        hi, lo = split(lt * jnp.concatenate([w, w], axis=1))
        x_v[pl.ds(0, CH), pl.ds(k * A, A)] = hi
        x_v[pl.ds(CH, CH), pl.ds(k * A, A)] = lo
    both = fast_dot(x_v[...], ah_own[...])
    message = both[:CH] + both[CH:] + fast_dot(x_v[pl.ds(0, CH), :], al_own[...])
    for copy in third:
        copy.wait_recv()
    ltg = jnp.transpose(l_v[pl.ds(A, 2 * G), :])
    for k in range(NB):
        hi, lo = split(ltg * w1bc[k])
        xg_v[pl.ds(0, CH), pl.ds(k * 2 * G, 2 * G)] = hi
        xg_v[pl.ds(CH, CH), pl.ds(k * 2 * G, 2 * G)] = lo
    both = fast_dot(xg_v[...], ah_gh[...])
    message = message + (both[:CH] + both[CH:] + fast_dot(xg_v[pl.ds(0, CH), :], al_gh[...]))
    u1 = exact_dot(wu1t[...], message)
    sig1 = 1.0 / (1.0 + jnp.exp(-u1))
    wo2 = jnp.concatenate([wocol[...], wocol[...]], axis=1)
    gu1 = wo2 * (sig1 * (1.0 + u1 * (1.0 - sig1)))
    gm1t = exact_dot(wu_v[1], gu1)
    gm_hi, gm_lo = split(jnp.transpose(gm1t))
    gcat = jnp.concatenate([gm_hi, gm_lo], axis=1)

    def feature_grad(ah, al, local):
        total = None
        for k in range(NB):
            y = fast_dot(ah[pl.ds(k * local, local), :], gcat)
            y2 = fast_dot(al[pl.ds(k * local, local), :], gm_hi)
            term = (w1[k : k + 1, :]) * (y[:, :CH] + y[:, CH:] + y2)
            total = term if total is None else total + term
        return total

    dl_gh[...] = feature_grad(ah_gh, al_gh, 2 * G)
    fourth = [
        side_copy(dl_gh.at[pl.ds(0, G)], r4_v.at[pl.ds(0, G)], s4.at[0], r4.at[0], right),
        side_copy(dl_gh.at[pl.ds(G, G)], r4_v.at[pl.ds(G, G)], s4.at[1], r4.at[1], left),
    ]
    for copy in fourth:
        copy.start()
    dl_own[...] = feature_grad(ah_own, al_own, A)
    l_hi, l_lo = split(l_v[...])
    lcat = jnp.concatenate([l_hi, l_lo], axis=1)
    for k in range(NB):
        w = w1bc[k]
        hi, lo = split(gm1t * jnp.concatenate([w, w], axis=1))
        da = fast_dot(lcat, jnp.concatenate([hi, hi], axis=0)) + fast_dot(l_hi, lo)
        term = da * z_v[pl.ds(k * E, E), :]
        q_v[...] = term if k == 0 else q_v[...] + term
    for copy in fourth:
        copy.wait_recv()
    dl_own[pl.ds(0, G), :] = dl_own[pl.ds(0, G), :] + r4_v[pl.ds(0, G), :]
    dl_own[pl.ds(A - G, G), :] = dl_own[pl.ds(A - G, G), :] + r4_v[pl.ds(G, G), :]
    gh1 = wo_v[...] + exact_dot_nt(dl_own[...], wm_v[1])
    gu0 = gh1 * slope0[...]
    db = exact_dot_nt(p0[...], gu0)
    base_rows = db[0:NB]
    both_rows = db[0:NB] + db[NB : 2 * NB]

    factor = -2.0 / (0.2 * ROOT)

    def force_rows(start):
        rows = 16

        def step(i, carry):
            base = pl.multiple_of(start + i * rows, rows)
            col = gcol[pl.ds(base, rows), :]
            kind = jnp.broadcast_to(col[:, 3:4], (rows, A)) > 0.5
            q = q_v[pl.ds(base, rows), :]
            for k in range(NB):
                coef = jnp.where(kind, both_rows[k : k + 1, :], base_rows[k : k + 1, :])
                q = q + coef * z_v[pl.ds(k * E + base, rows), :]
            g = q * rinv_v[pl.ds(base, rows), :] * factor
            new = []
            for c in range(3):
                f = g * (col[:, c : c + 1] - cen[c : c + 1, :])
                fold_v[c, pl.ds(base, rows), :] = f[:, :H] + f[:, H:]
                new.append(carry[c] + (f[0:8] + f[8:16]))
            return tuple(new)

        return step

    def row_sums(start):
        return jnp.concatenate(
            [jnp.sum(jnp.transpose(fold_v[c, pl.ds(start, H), :]), axis=0, keepdims=True)
             for c in range(3)], axis=0)

    pulls = tuple(jnp.zeros((8, A), F32) for _ in range(3))
    pulls = lax.fori_loop(0, 2 * G // 16, force_rows(A), pulls)
    tx5[...] = row_sums(A)
    fifth = [
        side_copy(tx5, r5_l, s5.at[0], r5.at[0], right),
        side_copy(tx5, r5_r, s5.at[1], r5.at[1], left),
    ]
    for copy in fifth:
        copy.start()
    pulls = lax.fori_loop(0, A // 16, force_rows(0), pulls)
    centre = jnp.concatenate([jnp.sum(v, axis=0, keepdims=True) for v in pulls], axis=0)
    lower = centre[:, :H] - row_sums(0)
    upper = centre[:, H:] - row_sums(H)
    for copy in fifth:
        copy.wait_recv()
    lower = lower - jnp.where(low, r5_l[...], 0.0)
    upper = upper - jnp.where(low, 0.0, r5_r[...])
    pull = jnp.concatenate([lower, upper], axis=0)
    tx6[...] = pull
    last = [None] + [
        bead_copy(tx6, rx6.at[lag], s6.at[lag], r6.at[lag], lag) for lag in range(1, nb)
    ]
    for lag in range(1, nb):
        last[lag].start()
    ratio = beads / reduced
    totals = [ratio * table_value(-j, beads, reduced) * pull for j in range(own)]
    for lag in range(1, nb):
        last[lag].wait_recv()
        arrived = rx6[lag]
        for j in range(own):
            totals[j] = totals[j] + ratio * table_value(-own * lag - j, beads, reduced) * arrived
    for c in range(3):
        for half in range(2):
            row = 3 * half + c
            out_ref[c, :, half * H : half * H + H] = jnp.concatenate(
                [totals[j][row : row + 1] for j in range(own)], axis=0)
    for copy in first[1:] + aux + second + third + fourth + fifth + last[1:]:
        copy.wait_send()


def solution(mesh):
    nb, ns = mesh.shape["bead"], mesh.shape["space"]

    def on_device(positions, species, neighbors, counts, send_rows, embed, w_radial, w_msg, w_upd, w_out):
        own = positions.shape[0]
        vm = pltpu.VMEM
        dma = pltpu.SemaphoreType.DMA
        scratch = [
            vm((3, own, A), F32), vm((2, H), jnp.int32), vm((K, A), jnp.int32), vm((1, A), jnp.int32),
            vm((1, H), jnp.int32), vm((2, CH), F32), vm((2, NB, CH), F32), vm((2, CH, CH), F32),
            vm((2, CH, CH), F32), vm((1, CH), F32),
            vm((nb, 6, H), F32), vm((nb, 6, H), F32), vm((2, H), jnp.int32), vm((2, H), jnp.int32),
            vm((1, H), jnp.int32), vm((1, H), jnp.int32), vm((6, H), F32), vm((6, H), F32), vm((6, H), F32),
            vm((K, A), jnp.int32), vm((E, A), F32), vm((E, H), F32), vm((8, A), F32), vm((NB, CH, H), F32),
            vm((CH, CH), F32), vm((CH, CH), F32), vm((2 * NB, CH), F32), vm((16 * NB, CH), F32),
            vm((A, CH), F32), vm((A, CH), F32),
            vm((NB * A, A), BF16), vm((NB * A, A), BF16), vm((NB * 2 * G, A), BF16), vm((NB * 2 * G, A), BF16),
            vm((NB * E, A), F32), vm((E, A), F32), vm((E, CH), F32), vm((2 * CH, NB * A), BF16),
            vm((2 * CH, NB * 2 * G), BF16), vm((E, A), F32), vm((A, CH), F32), vm((2 * G, CH), F32),
            vm((2 * G, CH), F32),
            vm((3, E, H), F32), vm((3, H), F32), vm((3, H), F32), vm((3, H), F32), vm((6, H), F32),
            vm((nb, 6, H), F32),
            dma((10,)), dma((nb,)), dma((nb,)), dma((4,)), dma((4,)), dma((2,)), dma((2,)), dma((2,)), dma((2,)),
            dma((2,)), dma((2,)), dma((2,)), dma((2,)), dma((nb,)), dma((nb,)),
        ]
        forces = pl.pallas_call(
            functools.partial(kernel, nb, ns, own),
            out_shape=jax.ShapeDtypeStruct((3, own, A), F32),
            in_specs=[pl.BlockSpec(memory_space=pl.ANY)] * 10,
            out_specs=pl.BlockSpec(memory_space=pltpu.VMEM),
            scratch_shapes=scratch,
            compiler_params=pltpu.CompilerParams(collective_id=0, has_side_effects=True),
        )(
            positions.transpose(1, 0, 2), species.reshape(2, H), neighbors, counts.reshape(1, A), send_rows.reshape(1, H),
            embed, w_radial, w_msg, w_upd, w_out.reshape(1, CH),
        )
        return forces.transpose(1, 0, 2)

    return jax.shard_map(
        on_device,
        mesh=mesh,
        in_specs=(
            P("bead", None, "space"), P("space"), P(None, "space"), P("space"), P("space"),
            P(), P(), P(), P(), P(),
        ),
        out_specs=P("bead", None, "space"),
        check_vma=False,
    )
```

time: 226 us -> 43 us (0.19)
  the two profiles are of different devices: /device:TPU:64 before, /device:TPU:2 now
where the time goes in v1:
time: 43 us; the launch traced here: 42.8 us
  Pallas kernels  41.5 us (97%)
  local copies, waits for them, and re-layouts  1.31 us (3%)
    pallas_call x1, Pallas kernels, on_device(): pl.pallas_call(functools.partial(kernel, nb, ns, own), out_shape=jax.Shap...  41.5 us
    unnamed x1, local copies, waits for them, and re-layouts  1.31 us

profile of v1, /device:TPU:2, one launch (start us, length us, event | category | flops | bytes accessed | tf_op | source)
XLA Modules:
  0.0 42.8 jit_solution(10684944197043123340)
XLA Ops:
  0.0 41.5 %shard_map.100 = f32[3,4,256]{2,1,0:T(4,128)} custom-call(f32[3,4,256]{2,1,0:T(4,128)} %bitcast.7, s32[2,128]{1,0:T(2,128)} %bitcast.8, s32[32,256]{1,0:T(8,128)} %nbr_h.1, s32[1,256]{1,0:T(1,128)} %bitcast.9, s32[1,128]{1,0:T(1,128)} %bitcast.10, f32[2,128]{1,0:T(2,128)} %emb_h.1, f32[2,8,128]{2,1,0:T(8,128)} %wr_h.1, f32[2,128,128]{2,1,0:T(8,128)} %wm_h.1, ...), custom_call_target="tpu_custom_call" | custom-call | tf_op jit(solution)/shard_map/pallas_call | solution.py:411
  41.5 1.3 %copy.12 = f32[4,3,256]{2,0,1:T(4,128)} copy(f32[4,3,256]{2,0,1:T(4,128)} %bitcast.6) | data formatting | bytes 24576

commit v2 on v1

v2 whole, which is shorter than its diff:
```python
import functools
import math

import jax
import jax.numpy as jnp
from jax import lax
from jax.experimental import pallas as pl
from jax.experimental.pallas import tpu as pltpu
from jax.sharding import PartitionSpec as P

MESH = pl.DeviceIdType.MESH
HI = lax.Precision.HIGHEST
F32 = jnp.float32
BF16 = jnp.bfloat16

NB = 8
CH = 128
A = 256
G = 64
E = A + 2 * G
K = 32
H = 128
ROOT = math.sqrt(math.log2(math.e))
STEP = ROOT / 0.2
CENTERS = tuple(STEP * 1.5 * b / (NB - 1) for b in range(NB))
FLOOR = 0.01
UNROLL = 2


def by_distance(nb):
    def far(lag):
        dz, dx = lag % 4, lag // 4
        return -(2 * min(dz, 4 - dz) + min(dx, 4 - dx))

    return sorted(range(1, nb), key=far)


def table_value(lag, beads, reduced):
    t = lag / beads
    total = 1.0 + math.cos(math.pi * reduced * t)
    for m in range(1, reduced // 2):
        total += 2.0 * math.cos(2.0 * math.pi * m * t)
    return total / beads


def split(v):
    hi = v.astype(BF16)
    lo = (v - hi.astype(F32)).astype(BF16)
    return hi, lo


def exact_dot(a, b):
    return jnp.dot(a, b, precision=HI, preferred_element_type=F32)


def fast_dot(a, b):
    return jnp.dot(a, b, preferred_element_type=F32)


def fast_dot_nt(a, b):
    return lax.dot_general(a, b, (((1,), (1,)), ((), ())), preferred_element_type=F32)


def kernel(
    nb, ns, own,
    pos_h, spc_h, nbr_h, cnt_h, snd_h, emb_h, wr_h, wm_h, wu_h, wo_h,
    out_ref,
    pos_v, spc_v, nbr_v, cnt_v, snd_v, emb_v, wr_v, wm_v, wu_v, wo_v,
    tx1, rx1,
    spc_r, snd_r, cnt_r, nbr_r, spc_l, snd_l, cnt_l, nbr_l, spc_rr, snd_rr, spc_ll, snd_ll,
    red_v, red_r, red_l, red_rr, red_ll,
    idx_v, idx_g, cnt_mat, cnt_gh, gb, ggb, cen, ceng, w1bc, wocol,
    p0r_hh, p0r_lo, p0_cat, wm_hh, wm_lo, wmt_hh, wmt_lo, wu_cat, wut_cat,
    h0_v, slope0, ah_v, al_v, z_v, zg_v, rinv_v, rinvg_v, x_v, q_v,
    dbs, fold_v, foldg_v, tx_r, tx_l, tx_rr, tx_ll, rx_r, rx_l, rx_rr, rx_ll, tx6, rx6,
    load_sem, s1, r1, sa, ra, s2, r2, s5, r5, s6, r6,
):
    beads, reduced = nb * own, nb
    scale = K ** -0.5
    b = lax.axis_index("bead")
    d = lax.axis_index("space")
    left = lax.rem(d + (ns - 1), ns)
    right = lax.rem(d + 1, ns)
    left2 = lax.rem(d + (ns - 2), ns)
    right2 = lax.rem(d + 2, ns)
    peers = [lax.rem(b + lag, nb) for lag in range(nb)]
    lags = by_distance(nb)

    def bead_copy(src, dst, ss, rs, lag):
        return pltpu.make_async_remote_copy(
            src_ref=src, dst_ref=dst, send_sem=ss, recv_sem=rs,
            device_id={"bead": peers[lag]}, device_id_type=MESH)

    def side_copy(src, dst, ss, rs, side):
        return pltpu.make_async_remote_copy(
            src_ref=src, dst_ref=dst, send_sem=ss, recv_sem=rs,
            device_id={"space": side}, device_id_type=MESH)

    barrier = pltpu.get_barrier_semaphore()
    for lag in lags:
        pl.semaphore_signal(barrier, inc=1, device_id={"bead": peers[lag]}, device_id_type=MESH)
    for side in (left, right, left2, right2):
        pl.semaphore_signal(barrier, inc=1, device_id={"space": side}, device_id_type=MESH)

    loads = []
    for i, (src, dst) in enumerate((
        (pos_h, pos_v), (spc_h, spc_v), (snd_h, snd_v), (nbr_h, nbr_v), (cnt_h, cnt_v),
        (emb_h, emb_v), (wr_h, wr_v), (wm_h, wm_v), (wu_h, wu_v), (wo_h, wo_v),
    )):
        copy = pltpu.make_async_copy(src, dst, load_sem.at[i])
        copy.start()
        loads.append(copy)

    loads[0].wait()
    packed = []
    for j in range(own):
        packed.append(jnp.concatenate(
            [pos_v[c, j : j + 1, half * H : half * H + H] for half in range(2) for c in range(3)], axis=0))
    for lag in range(nb):
        total = None
        for j in range(own):
            term = table_value(own * lag - j, beads, reduced) * packed[j]
            total = term if total is None else total + term
        tx1[lag] = total
    for copy in loads[1:5]:
        copy.wait()
    pl.semaphore_wait(barrier, nb + 3)

    first = {lag: bead_copy(tx1.at[lag], rx1.at[lag], s1.at[lag], r1.at[lag], lag) for lag in lags}
    for lag in lags:
        first[lag].start()
    near = pl.ds(0, H)
    far = pl.ds(H, H)
    aux = [
        side_copy(src, dst, sa.at[i], ra.at[i], side)
        for i, (src, dst, side) in enumerate((
            (nbr_v.at[:, near], nbr_r, left), (nbr_v.at[:, far], nbr_l, right),
            (cnt_v, cnt_r, left), (cnt_v, cnt_l, right),
            (spc_v, spc_r, left), (spc_v, spc_l, right), (spc_v, spc_rr, left2), (spc_v, spc_ll, right2),
            (snd_v, snd_r, left), (snd_v, snd_l, right), (snd_v, snd_rr, left2), (snd_v, snd_ll, right2),
        ))
    ]
    for copy in aux:
        copy.start()

    def rows_named(n, count):
        n = jnp.where(n >= A + G, n - G, jnp.where(n >= A, n + G, n))
        slot = lax.broadcasted_iota(jnp.int32, n.shape, 0)
        return jnp.where(slot < count, n, -1)

    def count_rows(idx, mat, width, rows):
        def step(i, carry):
            base = pl.multiple_of(i * rows, rows)
            row = lax.broadcasted_iota(jnp.int32, (rows, width), 0) + base
            acc = jnp.zeros((rows, width), F32)
            for k in range(K):
                acc = acc + jnp.where(idx[k : k + 1, :] == row, 1.0, 0.0)
            mat[pl.ds(base, rows), :] = acc
            return carry

        lax.fori_loop(0, E // rows, step, 0)

    idx_v[...] = rows_named(nbr_v[...], jnp.concatenate([cnt_v[0:1, :], cnt_v[1:2, :]], axis=1))
    count_rows(idx_v, cnt_mat, A, 32)

    for copy in loads[5:]:
        copy.wait()
    zeros6 = jnp.zeros((6, CH), F32)
    emb8 = jnp.concatenate([emb_v[...], zeros6], axis=0)
    table = exact_dot(emb8, wm_v[0])
    w0 = wr_v[0] * scale
    rows0 = jnp.concatenate([w0 * table[0:1], w0 * (table[1:2] - table[0:1])], axis=0)
    p0 = exact_dot(rows0, wu_v[0])
    p0_hi, p0_lo = split(p0)
    p0_cat[...] = jnp.concatenate([p0_hi, p0_lo], axis=1)
    hi, lo = split(jnp.concatenate(
        [jnp.broadcast_to(p0[j : j + 1, :], (8, CH)) for j in range(2 * NB)], axis=0))
    p0r_hh[...] = jnp.concatenate([hi, hi], axis=0)
    p0r_lo[...] = lo
    w1 = wr_v[1] * scale
    w1t = jnp.transpose(jnp.concatenate([w1, jnp.zeros((CH - NB, CH), F32)], axis=0))
    for k in range(NB):
        w1bc[k] = jnp.broadcast_to(w1t[:, k : k + 1], (CH, H))
    hi, lo = split(wm_v[1])
    wm_hh[...] = jnp.concatenate([hi, hi], axis=0)
    wm_lo[...] = lo
    hi, lo = split(jnp.transpose(wm_v[1]))
    wmt_hh[...] = jnp.concatenate([hi, hi], axis=0)
    wmt_lo[...] = lo
    hi, lo = split(wu_v[1])
    wu_cat[...] = jnp.concatenate([hi, lo], axis=1)
    hi, lo = split(jnp.transpose(wu_v[1]))
    wut_cat[...] = jnp.concatenate([hi, lo], axis=1)
    wocol[...] = jnp.transpose(jnp.broadcast_to(wo_v[...], (CH, CH)))

    lane = lax.broadcasted_iota(jnp.int32, (1, H), 1)
    low = lane < G

    red = tx1[0]
    for lag in lags:
        first[lag].wait_recv()
        red = red + rx1[lag]
    red_v[...] = red
    second = [
        side_copy(red_v, dst, s2.at[i], r2.at[i], side)
        for i, (dst, side) in enumerate(((red_r, left), (red_l, right), (red_rr, left2), (red_ll, right2)))
    ]
    for copy in second:
        copy.start()

    for copy in aux:
        copy.wait_recv()
    idx_g[...] = rows_named(
        jnp.where(low, nbr_r[...], nbr_l[...]), jnp.where(low, cnt_r[0:1, :], cnt_l[1:2, :]))
    count_rows(idx_g, cnt_gh, H, 64)
    natural = lax.broadcasted_iota(jnp.int32, (H, H), 0)

    def reorder(from_right, from_left, rows):
        order = jnp.where(low, from_right, from_left - (A - H))
        return fast_dot(jnp.where(natural == order, 1.0, 0.0).astype(BF16), rows)

    cnt_mat[pl.ds(A, 2 * G), :] = reorder(snd_r[...], snd_l[...], cnt_mat[pl.ds(A, 2 * G), :].astype(BF16))
    rows_gh = cnt_gh[pl.ds(A, 2 * G), :].astype(BF16)
    cnt_gh[pl.ds(A, 2 * G), :] = jnp.where(
        low, reorder(snd_rr[...], snd_v[...], rows_gh), reorder(snd_v[...], snd_ll[...], rows_gh))
    kind_own = spc_v[...].astype(F32)
    kind_r, kind_l = spc_r[...].astype(F32), spc_l[...].astype(F32)
    kind_gh = jnp.where(low, kind_r[0:1], kind_l[1:2])
    kind_rg = jnp.where(low, spc_rr[0:1, :].astype(F32), kind_own[1:2])
    kind_lg = jnp.where(low, kind_own[0:1], spc_ll[1:2, :].astype(F32))
    zrest = jnp.zeros((CH - 4, H), F32)
    z3 = jnp.zeros((3, H), F32)
    for part, kind in enumerate((kind_own[0:1], kind_own[1:2], kind_gh)):
        kcol = jnp.transpose(jnp.concatenate([z3, kind, zrest], axis=0))
        h0_v[pl.ds(part * H, H), :] = jnp.where(kcol[:, 3:4] > 0.5, emb_v[1:2, :], emb_v[0:1, :])
    cen[...] = jnp.concatenate(
        [jnp.concatenate([red[0:3], red[3:6]], axis=1), jnp.zeros((5, A), F32)], axis=0)

    def spread_rows(part, pieces):
        col = jnp.transpose(jnp.concatenate(pieces + [zrest], axis=0))
        for c in range(4):
            gb[c, pl.ds(part * H, H), :] = jnp.broadcast_to(col[:, c : c + 1], (H, H))

    for half in range(2):
        spread_rows(half, [red[3 * half : 3 * half + 3], kind_own[half : half + 1]])

    def folded(v):
        total = v[0:8]
        for r in range(8, v.shape[0], 8):
            total = total + v[r : r + 8]
        return total

    def pair_rows(start):
        rows = 16

        def step(i, carry):
            base = pl.multiple_of(start + i * rows, rows)
            at = pl.ds(base, rows)
            gx, gy, gz, kind = [gb[c, at, :] for c in range(4)]
            sums = list(carry)
            for half in range(2):
                lanes = pl.ds(half * H, H)
                dx, dy, dz = gx - cen[0:1, lanes], gy - cen[1:2, lanes], gz - cen[2:3, lanes]
                square = dx * dx + dy * dy + dz * dz + FLOOR
                rinv = lax.rsqrt(square)
                x = square * rinv * STEP
                rinv_v[at, lanes] = rinv
                c = cnt_mat[at, lanes]
                for k in range(NB):
                    off = x - CENTERS[k]
                    a = c * jnp.exp2(-(off * off))
                    hi, lo = split(a)
                    ah_v[pl.ds(k * E + base, rows), lanes] = hi
                    al_v[pl.ds(k * E + base, rows), lanes] = lo
                    z_v[pl.ds(k * E + base, rows), lanes] = a * off
                    sums[2 * k + half] = sums[2 * k + half] + folded(a)
                    j = 2 * NB + 2 * k + half
                    sums[j] = sums[j] + folded(a * kind)
            return tuple(sums)

        return step

    sums = tuple(jnp.zeros((8, H), F32) for _ in range(4 * NB))
    sums = lax.fori_loop(0, A // 16, pair_rows(0), sums, unroll=UNROLL)
    for copy in second:
        copy.wait_recv()

    def shifted(at_left, at_right, values):
        shift = jnp.where(low, jnp.where(at_right, float(ns), 0.0), jnp.where(at_left, -float(ns), 0.0))
        first_row = lax.broadcasted_iota(jnp.int32, (3, H), 0) == 0
        return values + jnp.where(first_row, shift, 0.0)

    borrowed = jnp.where(low, red_r[0:3, :], red_l[3:6, :])
    ceng[...] = jnp.concatenate([borrowed, jnp.zeros((5, H), F32)], axis=0)
    ghost = shifted(d == 0, d == ns - 1, borrowed)
    ghost_r = shifted(right == 0, right == ns - 1, jnp.where(low, red_rr[0:3, :], red[3:6]))
    ghost_l = shifted(left == 0, left == ns - 1, jnp.where(low, red[0:3], red_ll[3:6, :]))
    spread_rows(2, [ghost, kind_gh])
    zrest8 = jnp.zeros((CH - 8, H), F32)
    for part, pieces in enumerate((
        (red_r[0:3, :], kind_r[0:1], red_l[0:3, :], kind_l[0:1]),
        (red_r[3:6, :], kind_r[1:2], red_l[3:6, :], kind_l[1:2]),
        (ghost_r, kind_rg, ghost_l, kind_lg),
    )):
        col = jnp.transpose(jnp.concatenate(list(pieces) + [zrest8], axis=0))
        for c in range(4):
            ggb[c, pl.ds(part * H, H), :] = jnp.where(low, col[:, c : c + 1], col[:, c + 4 : c + 5])

    def ghost_rows(i, carry):
        rows = 32
        base = pl.multiple_of(i * rows, rows)
        dx, dy, dz = [ggb[c, pl.ds(base, rows), :] - ceng[c : c + 1, :] for c in range(3)]
        kind = ggb[3, pl.ds(base, rows), :]
        square = dx * dx + dy * dy + dz * dz + FLOOR
        rinv = lax.rsqrt(square)
        x = square * rinv * STEP
        rinvg_v[pl.ds(base, rows), :] = rinv
        c = cnt_gh[pl.ds(base, rows), :]
        sums = list(carry)
        for k in range(NB):
            off = x - CENTERS[k]
            a = c * jnp.exp2(-(off * off))
            zg_v[pl.ds(k * E + base, rows), :] = a * off
            s = a * kind
            sums[k] = sums[k] + folded(a)
            sums[NB + k] = sums[NB + k] + folded(s)
        return tuple(sums)

    sums = lax.fori_loop(0, 2 * G // 16, pair_rows(A), sums, unroll=UNROLL)
    gsums = tuple(jnp.zeros((8, H), F32) for _ in range(2 * NB))
    gsums = lax.fori_loop(0, E // 32, ghost_rows, gsums, unroll=UNROLL)

    stacked = jnp.concatenate(
        [jnp.concatenate(sums[0::2], axis=0), jnp.concatenate(sums[1::2], axis=0),
         jnp.concatenate(gsums, axis=0)], axis=1)
    hi, lo = split(jnp.transpose(stacked))
    u0 = fast_dot(jnp.concatenate([hi, lo], axis=1), p0r_hh[...]) + fast_dot(hi, p0r_lo[...])
    sig0 = 1.0 / (1.0 + jnp.exp(-u0))
    slope0[...] = sig0 * (1.0 + u0 * (1.0 - sig0))
    hi, lo = split(h0_v[...] + u0 * sig0)
    lent = fast_dot(jnp.concatenate([hi, lo], axis=1), wm_hh[...]) + fast_dot(hi, wm_lo[...])

    lt = jnp.transpose(lent)
    for k in range(NB):
        w = w1bc[k]
        hi, lo = split(lt * jnp.concatenate([w, w, w], axis=1))
        x_v[pl.ds(0, CH), pl.ds(k * E, E)] = hi
        x_v[pl.ds(CH, CH), pl.ds(k * E, E)] = lo
    both = fast_dot(x_v[...], ah_v[...])
    message = both[:CH] + both[CH:] + fast_dot(x_v[pl.ds(0, CH), :], al_v[...])
    hi, lo = split(message)
    wut = wut_cat[...]
    u1 = fast_dot(wut, jnp.concatenate([hi, hi], axis=0)) + fast_dot(wut[:, :CH], lo)
    sig1 = 1.0 / (1.0 + jnp.exp(-u1))
    wo2 = jnp.concatenate([wocol[...], wocol[...]], axis=1)
    hi, lo = split(wo2 * (sig1 * (1.0 + u1 * (1.0 - sig1))))
    wu = wu_cat[...]
    gm1t = fast_dot(wu, jnp.concatenate([hi, hi], axis=0)) + fast_dot(wu[:, :CH], lo)
    gm_hi, gm_lo = split(jnp.transpose(gm1t))
    gcat = jnp.concatenate([gm_hi, gm_lo], axis=1)
    dl = None
    for k in range(NB):
        y = fast_dot(ah_v[pl.ds(k * E, E), :], gcat)
        y2 = fast_dot(al_v[pl.ds(k * E, E), :], gm_hi)
        term = w1[k : k + 1, :] * (y[:, :CH] + y[:, CH:] + y2)
        dl = term if dl is None else dl + term
    hi, lo = split(dl)
    gh1 = fast_dot(jnp.concatenate([hi, lo], axis=1), wmt_hh[...]) + fast_dot(hi, wmt_lo[...])
    gh1 = jnp.concatenate([gh1[:A] + wo_v[...], gh1[A:]], axis=0)
    hi, lo = split(gh1 * slope0[...])
    p0c = p0_cat[...]
    db = fast_dot_nt(p0c, jnp.concatenate([hi, hi], axis=1)) + fast_dot_nt(p0c[:, :CH], lo)
    dbs[...] = jnp.concatenate([db[0:NB], db[0:NB] + db[NB : 2 * NB]], axis=0)
    l_hi, l_lo = split(lent)
    lcat = jnp.concatenate([l_hi, l_lo], axis=1)
    for k in range(NB):
        w = w1bc[k]
        hi, lo = split(gm1t * jnp.concatenate([w, w], axis=1))
        da = fast_dot(lcat, jnp.concatenate([hi, hi], axis=0)) + fast_dot(l_hi, lo)
        term = da * z_v[pl.ds(k * E, E), :]
        q_v[...] = term if k == 0 else q_v[...] + term

    factor = -2.0 / (0.2 * ROOT)

    def force_rows(start):
        rows = 16

        def step(i, carry):
            base = pl.multiple_of(start + i * rows, rows)
            at = pl.ds(base, rows)
            kind = gb[3, at, :] > 0.5
            new = list(carry)
            folds = [None] * 3
            for half in range(2):
                lanes = pl.ds(half * H, H)
                q = q_v[at, lanes]
                for k in range(NB):
                    coef = jnp.where(kind, dbs[NB + k : NB + k + 1, lanes], dbs[k : k + 1, lanes])
                    q = q + coef * z_v[pl.ds(k * E + base, rows), lanes]
                g = q * rinv_v[at, lanes] * factor
                for c in range(3):
                    f = g * (gb[c, at, :] - cen[c : c + 1, lanes])
                    folds[c] = f if half == 0 else folds[c] + f
                    new[2 * c + half] = new[2 * c + half] + folded(f)
            for c in range(3):
                fold_v[c, at, :] = folds[c]
            return tuple(new)

        return step

    def ghost_force(i, carry):
        rows = 32
        base = pl.multiple_of(i * rows, rows)
        kind = ggb[3, pl.ds(base, rows), :] > 0.5
        q = None
        for k in range(NB):
            coef = jnp.where(kind, dbs[NB + k : NB + k + 1, A:], dbs[k : k + 1, A:])
            term = coef * zg_v[pl.ds(k * E + base, rows), :]
            q = term if q is None else q + term
        g = q * rinvg_v[pl.ds(base, rows), :] * factor
        new = []
        for c in range(3):
            f = g * (ggb[c, pl.ds(base, rows), :] - ceng[c : c + 1, :])
            foldg_v[c, pl.ds(base, rows), :] = f
            new.append(carry[c] + folded(f))
        return tuple(new)

    def row_sums(start):
        return jnp.concatenate(
            [jnp.sum(jnp.transpose(fold_v[c, pl.ds(start, H), :]), axis=0, keepdims=True)
             for c in range(3)], axis=0)

    def ghost_sums(start):
        turned = [jnp.transpose(foldg_v[c, pl.ds(start, H), :]) for c in range(3)]
        return [
            jnp.concatenate([jnp.sum(t[G * part : G * part + G], axis=0, keepdims=True) for t in turned], axis=0)
            for part in range(2)
        ]

    gpulls = tuple(jnp.zeros((8, H), F32) for _ in range(3))
    gpulls = lax.fori_loop(0, E // 32, ghost_force, gpulls, unroll=UNROLL)
    pulls = tuple(jnp.zeros((8, H), F32) for _ in range(6))
    pulls = lax.fori_loop(0, 2 * G // 16, force_rows(A), pulls, unroll=UNROLL)
    lent_pull = row_sums(A) - jnp.concatenate([jnp.sum(v, axis=0, keepdims=True) for v in gpulls], axis=0)
    r_low, l_low = ghost_sums(0)
    r_high, l_high = ghost_sums(H)
    r_end, l_end = ghost_sums(2 * H)
    tx_r[...] = jnp.concatenate([r_low + jnp.where(low, lent_pull, 0.0), r_high], axis=0)
    tx_l[...] = jnp.concatenate([l_low, l_high + jnp.where(low, 0.0, lent_pull)], axis=0)
    tx_rr[...] = r_end
    tx_ll[...] = l_end
    fifth = [
        side_copy(src, dst, s5.at[i], r5.at[i], side)
        for i, (src, dst, side) in enumerate((
            (tx_r, rx_l, right), (tx_l, rx_r, left), (tx_rr, rx_ll, right2), (tx_ll, rx_rr, left2)))
    ]
    for copy in fifth:
        copy.start()
    pulls = lax.fori_loop(0, A // 16, force_rows(0), pulls, unroll=UNROLL)
    centre = [jnp.sum(v, axis=0, keepdims=True) for v in pulls]
    lower = jnp.concatenate(centre[0::2], axis=0) - row_sums(0) - jnp.where(low, l_end, 0.0)
    upper = jnp.concatenate(centre[1::2], axis=0) - row_sums(H) - jnp.where(low, 0.0, r_end)
    for copy in fifth:
        copy.wait_recv()
    lower = lower - jnp.where(low, rx_ll[...], 0.0)
    upper = upper - jnp.where(low, 0.0, rx_rr[...])
    pull = jnp.concatenate([lower, upper], axis=0) - (rx_l[...] + rx_r[...])
    tx6[...] = pull
    last = {lag: bead_copy(tx6, rx6.at[lag], s6.at[lag], r6.at[lag], lag) for lag in lags}
    for lag in lags:
        last[lag].start()
    ratio = beads / reduced
    totals = [ratio * table_value(-j, beads, reduced) * pull for j in range(own)]
    for lag in reversed(lags):
        last[lag].wait_recv()
        arrived = rx6[lag]
        for j in range(own):
            totals[j] = totals[j] + ratio * table_value(-own * lag - j, beads, reduced) * arrived
    for c in range(3):
        for half in range(2):
            row = 3 * half + c
            out_ref[c, :, half * H : half * H + H] = jnp.concatenate(
                [totals[j][row : row + 1] for j in range(own)], axis=0)
    for copy in list(first.values()) + aux + second + fifth + list(last.values()):
        copy.wait_send()


def solution(mesh):
    nb, ns = mesh.shape["bead"], mesh.shape["space"]

    def on_device(positions, species, neighbors, counts, send_rows, embed, w_radial, w_msg, w_upd, w_out):
        own = positions.shape[0]
        dma = pltpu.SemaphoreType.DMA

        def f32(*dims):
            return pltpu.VMEM(dims, F32)

        def i32(*dims):
            return pltpu.VMEM(dims, jnp.int32)

        def b16(*dims):
            return pltpu.VMEM(dims, BF16)

        scratch = [
            f32(3, own, A), i32(2, H), i32(K, A), i32(2, H), i32(1, H), f32(2, CH), f32(2, NB, CH),
            f32(2, CH, CH), f32(2, CH, CH), f32(1, CH),
            f32(nb, 6, H), f32(nb, 6, H),
            i32(2, H), i32(1, H), i32(2, H), i32(K, H), i32(2, H), i32(1, H), i32(2, H), i32(K, H),
            i32(2, H), i32(1, H), i32(2, H), i32(1, H),
            f32(6, H), f32(6, H), f32(6, H), f32(6, H), f32(6, H),
            i32(K, A), i32(K, H), f32(E, A), f32(E, H), f32(4, E, H), f32(4, E, H), f32(8, A), f32(8, H),
            f32(NB, CH, H), f32(CH, CH),
            b16(2 * CH, CH), b16(CH, CH), b16(2 * NB, 2 * CH), b16(2 * CH, CH), b16(CH, CH),
            b16(2 * CH, CH), b16(CH, CH), b16(CH, 2 * CH), b16(CH, 2 * CH),
            f32(E, CH), f32(E, CH), b16(NB * E, A), b16(NB * E, A), f32(NB * E, A), f32(NB * E, H),
            f32(E, A), f32(E, H), b16(2 * CH, NB * E), f32(E, A),
            f32(2 * NB, E), f32(3, E, H), f32(3, E, H),
            f32(6, H), f32(6, H), f32(3, H), f32(3, H), f32(6, H), f32(6, H), f32(3, H), f32(3, H),
            f32(6, H), f32(nb, 6, H),
            dma((10,)), dma((nb,)), dma((nb,)), dma((12,)), dma((12,)), dma((4,)), dma((4,)), dma((4,)), dma((4,)),
            dma((nb,)), dma((nb,)),
        ]
        forces = pl.pallas_call(
            functools.partial(kernel, nb, ns, own),
            out_shape=jax.ShapeDtypeStruct((3, own, A), F32),
            in_specs=[pl.BlockSpec(memory_space=pltpu.HBM)] * 10,
            out_specs=pl.BlockSpec(memory_space=pltpu.VMEM),
            scratch_shapes=scratch,
            compiler_params=pltpu.CompilerParams(
                collective_id=0, has_side_effects=True, vmem_limit_bytes=40 * 1024 * 1024),
        )(
            *[pltpu.with_memory_space_constraint(v, pltpu.HBM) for v in (positions.transpose(1, 0, 2), species.reshape(2, H), neighbors, counts.reshape(2, H),
            send_rows.reshape(1, H), embed, w_radial, w_msg, w_upd, w_out.reshape(1, CH))],
        )
        return forces.transpose(1, 0, 2)

    return jax.shard_map(
        on_device,
        mesh=mesh,
        in_specs=(
            P("bead", None, "space"), P("space"), P(None, "space"), P("space"), P("space"),
            P(), P(), P(), P(), P(),
        ),
        out_specs=P("bead", None, "space"),
        check_vma=False,
    )
```

time: 43 us -> 38.5 us (0.90)
  the two profiles are of different devices: /device:TPU:2 before, /device:TPU:24 now
where the time goes in v2:
time: 38.5 us; the launch traced here: 38.4 us
  Pallas kernels  37.7 us (98%)
  local copies, waits for them, and re-layouts  0.6 us (2%)
    pallas_call x1, Pallas kernels, on_device(): pl.pallas_call(functools.partial(kernel, nb, ns, own), out_shape=jax.Shap...  37.7 us

profile of v2, /device:TPU:24, one launch (start us, length us, event | category | flops | bytes accessed | tf_op | source)
XLA Modules:
  0.0 38.4 jit_solution(13571216765029627189)
XLA Ops:
  0.0 37.7 %shard_map.100 = f32[3,4,256]{2,1,0:T(4,128)S(1)} custom-call(f32[3,4,256]{2,1,0:T(4,128)} %bitcast.7, s32[2,128]{1,0:T(2,128)} %bitcast.8, s32[32,256]{1,0:T(8,128)} %nbr_h.1, s32[2,128]{1,0:T(2,128)} %bitcast.9, s32[1,128]{1,0:T(1,128)} %bitcast.10, f32[2,128]{1,0:T(2,128)} %emb_h.1, f32[2,8,128]{2,1,0:T(8,128)} %wr_h.1, f32[2,128,128]{2,1,0:T(8,128)} %wm_h.1, ...), custom_call_target="tpu_custom_call" | custom-call | tf_op jit(solution)/shard_map/pallas_call | solution.py:523
  37.8 0.6 %copy.12 = f32[4,3,256]{2,0,1:T(4,128)} copy(f32[4,3,256]{2,0,1:T(4,128)S(1)} %bitcast.6) | data formatting | bytes 24576

commit v3 on v2

--- a/solution.py
+++ b/solution.py
@@ -57,6 +57,18 @@
     return jnp.dot(a, b, preferred_element_type=F32)
 
 
+def wide(w):
+    hi, lo = split(w)
+    row = jnp.concatenate([hi, lo], axis=1)
+    return jnp.concatenate([row, row], axis=0)
+
+
+def wide_dot(a, w):
+    hi, lo = split(a)
+    both = fast_dot(jnp.concatenate([hi, lo], axis=1), w)
+    return both[:, :CH] + both[:, CH:]
+
+
 def fast_dot_nt(a, b):
     return lax.dot_general(a, b, (((1,), (1,)), ((), ())), preferred_element_type=F32)
 
@@ -70,9 +82,9 @@
     spc_r, snd_r, cnt_r, nbr_r, spc_l, snd_l, cnt_l, nbr_l, spc_rr, snd_rr, spc_ll, snd_ll,
     red_v, red_r, red_l, red_rr, red_ll,
     idx_v, idx_g, cnt_mat, cnt_gh, gb, ggb, cen, ceng, w1bc, wocol,
-    p0r_hh, p0r_lo, p0_cat, wm_hh, wm_lo, wmt_hh, wmt_lo, wu_cat, wut_cat,
-    h0_v, slope0, ah_v, al_v, z_v, zg_v, rinv_v, rinvg_v, x_v, q_v,
-    dbs, fold_v, foldg_v, tx_r, tx_l, tx_rr, tx_ll, rx_r, rx_l, rx_rr, rx_ll, tx6, rx6,
+    p0r_w, p0_cat, wm_w, wmt_w, wu_cat, wut_cat,
+    h0_v, slope0, ah_v, al_v, z_v, zg_v, rinv_v, rinvg_v, gs_v, q_v,
+    pick_v, dbs, fold_v, foldg_v, tx_r, tx_l, tx_rr, tx_ll, rx_r, rx_l, rx_rr, rx_ll, tx6, rx6,
     load_sem, s1, r1, sa, ra, s2, r2, s5, r5, s6, r6,
 ):
     beads, reduced = nb * own, nb
@@ -89,18 +101,18 @@
     def bead_copy(src, dst, ss, rs, lag):
         return pltpu.make_async_remote_copy(
             src_ref=src, dst_ref=dst, send_sem=ss, recv_sem=rs,
-            device_id={"bead": peers[lag]}, device_id_type=MESH)
+            device_id=peers[lag] * ns + d, device_id_type=pl.DeviceIdType.LOGICAL)
 
     def side_copy(src, dst, ss, rs, side):
         return pltpu.make_async_remote_copy(
             src_ref=src, dst_ref=dst, send_sem=ss, recv_sem=rs,
-            device_id={"space": side}, device_id_type=MESH)
+            device_id=b * ns + side, device_id_type=pl.DeviceIdType.LOGICAL)
 
     barrier = pltpu.get_barrier_semaphore()
     for lag in lags:
-        pl.semaphore_signal(barrier, inc=1, device_id={"bead": peers[lag]}, device_id_type=MESH)
+        pl.semaphore_signal(barrier, inc=1, device_id=peers[lag] * ns + d, device_id_type=pl.DeviceIdType.LOGICAL)
     for side in (left, right, left2, right2):
-        pl.semaphore_signal(barrier, inc=1, device_id={"space": side}, device_id_type=MESH)
+        pl.semaphore_signal(barrier, inc=1, device_id=b * ns + side, device_id_type=pl.DeviceIdType.LOGICAL)
 
     loads = []
     for i, (src, dst) in enumerate((
@@ -173,20 +185,14 @@
     p0 = exact_dot(rows0, wu_v[0])
     p0_hi, p0_lo = split(p0)
     p0_cat[...] = jnp.concatenate([p0_hi, p0_lo], axis=1)
-    hi, lo = split(jnp.concatenate(
+    p0r_w[...] = wide(jnp.concatenate(
         [jnp.broadcast_to(p0[j : j + 1, :], (8, CH)) for j in range(2 * NB)], axis=0))
-    p0r_hh[...] = jnp.concatenate([hi, hi], axis=0)
-    p0r_lo[...] = lo
     w1 = wr_v[1] * scale
     w1t = jnp.transpose(jnp.concatenate([w1, jnp.zeros((CH - NB, CH), F32)], axis=0))
     for k in range(NB):
         w1bc[k] = jnp.broadcast_to(w1t[:, k : k + 1], (CH, H))
-    hi, lo = split(wm_v[1])
-    wm_hh[...] = jnp.concatenate([hi, hi], axis=0)
-    wm_lo[...] = lo
-    hi, lo = split(jnp.transpose(wm_v[1]))
-    wmt_hh[...] = jnp.concatenate([hi, hi], axis=0)
-    wmt_lo[...] = lo
+    wm_w[...] = wide(wm_v[1])
+    wmt_w[...] = wide(jnp.transpose(wm_v[1]))
     hi, lo = split(wu_v[1])
     wu_cat[...] = jnp.concatenate([hi, lo], axis=1)
     hi, lo = split(jnp.transpose(wu_v[1]))
@@ -195,6 +201,11 @@
 
     lane = lax.broadcasted_iota(jnp.int32, (1, H), 1)
     low = lane < G
+
+    row = lax.broadcasted_iota(jnp.int32, (CH, 4 * H), 0)
+    spot = lax.broadcasted_iota(jnp.int32, (CH, 4 * H), 1)
+    value = spot // H + jnp.where(spot % H < G, 0, 4)
+    pick_v[...] = jnp.where((row < 24) & (row % 8 == value), 1.0, 0.0).astype(BF16)
 
     red = tx1[0]
     for lag in lags:
@@ -270,8 +281,9 @@
                     off = x - CENTERS[k]
                     a = c * jnp.exp2(-(off * off))
                     hi, lo = split(a)
-                    ah_v[pl.ds(k * E + base, rows), lanes] = hi
-                    al_v[pl.ds(k * E + base, rows), lanes] = lo
+                    spot = pl.ds(k * A + half * H, H)
+                    ah_v[at, spot] = hi
+                    al_v[at, spot] = lo
                     z_v[pl.ds(k * E + base, rows), lanes] = a * off
                     sums[2 * k + half] = sums[2 * k + half] + folded(a)
                     j = 2 * NB + 2 * k + half
@@ -296,15 +308,21 @@
     ghost_r = shifted(right == 0, right == ns - 1, jnp.where(low, red_rr[0:3, :], red[3:6]))
     ghost_l = shifted(left == 0, left == ns - 1, jnp.where(low, red[0:3], red_ll[3:6, :]))
     spread_rows(2, [ghost, kind_gh])
-    zrest8 = jnp.zeros((CH - 8, H), F32)
     for part, pieces in enumerate((
         (red_r[0:3, :], kind_r[0:1], red_l[0:3, :], kind_l[0:1]),
         (red_r[3:6, :], kind_r[1:2], red_l[3:6, :], kind_l[1:2]),
         (ghost_r, kind_rg, ghost_l, kind_lg),
     )):
-        col = jnp.transpose(jnp.concatenate(list(pieces) + [zrest8], axis=0))
+        rest = jnp.concatenate(list(pieces), axis=0)
+        layers = []
+        for _ in range(3):
+            layer = rest.astype(BF16).astype(F32)
+            layers.append(layer)
+            rest = rest - layer
+        col = jnp.transpose(jnp.concatenate(layers + [jnp.zeros((CH - 24, H), F32)], axis=0)).astype(BF16)
+        spread = fast_dot(col, pick_v[...])
         for c in range(4):
-            ggb[c, pl.ds(part * H, H), :] = jnp.where(low, col[:, c : c + 1], col[:, c + 4 : c + 5])
+            ggb[c, pl.ds(part * H, H), :] = spread[:, c * H : c * H + H]
 
     def ghost_rows(i, carry):
         rows = 32
@@ -333,21 +351,21 @@
     stacked = jnp.concatenate(
         [jnp.concatenate(sums[0::2], axis=0), jnp.concatenate(sums[1::2], axis=0),
          jnp.concatenate(gsums, axis=0)], axis=1)
-    hi, lo = split(jnp.transpose(stacked))
-    u0 = fast_dot(jnp.concatenate([hi, lo], axis=1), p0r_hh[...]) + fast_dot(hi, p0r_lo[...])
+    u0 = wide_dot(jnp.transpose(stacked), p0r_w[...])
     sig0 = 1.0 / (1.0 + jnp.exp(-u0))
     slope0[...] = sig0 * (1.0 + u0 * (1.0 - sig0))
-    hi, lo = split(h0_v[...] + u0 * sig0)
-    lent = fast_dot(jnp.concatenate([hi, lo], axis=1), wm_hh[...]) + fast_dot(hi, wm_lo[...])
+    lent = wide_dot(h0_v[...] + u0 * sig0, wm_w[...])
 
     lt = jnp.transpose(lent)
-    for k in range(NB):
-        w = w1bc[k]
-        hi, lo = split(lt * jnp.concatenate([w, w, w], axis=1))
-        x_v[pl.ds(0, CH), pl.ds(k * E, E)] = hi
-        x_v[pl.ds(CH, CH), pl.ds(k * E, E)] = lo
-    both = fast_dot(x_v[...], ah_v[...])
-    message = both[:CH] + both[CH:] + fast_dot(x_v[pl.ds(0, CH), :], al_v[...])
+    message = None
+    for k in range(0, NB, 2):
+        parts = [split(lt * jnp.concatenate([w1bc[m]] * 3, axis=1)) for m in (k, k + 1)]
+        hi, lo = [jnp.concatenate([part[j] for part in parts], axis=1) for j in range(2)]
+        a_hi, a_lo = [
+            jnp.concatenate([v[:, pl.ds(m * A, A)] for m in (k, k + 1)], axis=0) for v in (ah_v, al_v)]
+        both = fast_dot(jnp.concatenate([hi, lo], axis=0), a_hi)
+        term = both[:CH] + both[CH:] + fast_dot(hi, a_lo)
+        message = term if message is None else message + term
     hi, lo = split(message)
     wut = wut_cat[...]
     u1 = fast_dot(wut, jnp.concatenate([hi, hi], axis=0)) + fast_dot(wut[:, :CH], lo)
@@ -356,29 +374,38 @@
     hi, lo = split(wo2 * (sig1 * (1.0 + u1 * (1.0 - sig1))))
     wu = wu_cat[...]
     gm1t = fast_dot(wu, jnp.concatenate([hi, hi], axis=0)) + fast_dot(wu[:, :CH], lo)
-    gm_hi, gm_lo = split(jnp.transpose(gm1t))
-    gcat = jnp.concatenate([gm_hi, gm_lo], axis=1)
-    dl = None
+    gm1 = jnp.transpose(gm1t)
     for k in range(NB):
-        y = fast_dot(ah_v[pl.ds(k * E, E), :], gcat)
-        y2 = fast_dot(al_v[pl.ds(k * E, E), :], gm_hi)
-        term = w1[k : k + 1, :] * (y[:, :CH] + y[:, CH:] + y2)
-        dl = term if dl is None else dl + term
-    hi, lo = split(dl)
-    gh1 = fast_dot(jnp.concatenate([hi, lo], axis=1), wmt_hh[...]) + fast_dot(hi, wmt_lo[...])
+        hi, lo = split(gm1 * w1[k : k + 1, :])
+        gs_v[pl.ds(k * A, A), pl.ds(0, CH)] = hi
+        gs_v[pl.ds(k * A, A), pl.ds(CH, CH)] = lo
+    both = fast_dot(ah_v[...], gs_v[...])
+    both = both + fast_dot(al_v[...], gs_v[...])
+    dl = both[:, :CH] + both[:, CH:]
+    l_hi, l_lo = split(lent)
+    lcat = jnp.concatenate([l_hi, l_lo], axis=1)
+
+    def radial_grad(ks, rows):
+        for k in ks:
+            w = w1bc[k]
+            hi, lo = split(gm1t * jnp.concatenate([w, w], axis=1))
+            first_row, last_row = rows
+            da = fast_dot(lcat[first_row:last_row], jnp.concatenate([hi, hi], axis=0))
+            da = da + fast_dot(l_hi[first_row:last_row], lo)
+            at = pl.ds(first_row, last_row - first_row)
+            term = da * z_v[pl.ds(k * E + first_row, last_row - first_row), :]
+            q_v[at, :] = term if k == 0 else q_v[at, :] + term
+
+    ghosts = (A, E)
+    radial_grad((0, 1, 2), ghosts)
+    gh1 = wide_dot(dl, wmt_w[...])
+    radial_grad((3, 4, 5), ghosts)
     gh1 = jnp.concatenate([gh1[:A] + wo_v[...], gh1[A:]], axis=0)
     hi, lo = split(gh1 * slope0[...])
     p0c = p0_cat[...]
     db = fast_dot_nt(p0c, jnp.concatenate([hi, hi], axis=1)) + fast_dot_nt(p0c[:, :CH], lo)
+    radial_grad((6, 7), ghosts)
     dbs[...] = jnp.concatenate([db[0:NB], db[0:NB] + db[NB : 2 * NB]], axis=0)
-    l_hi, l_lo = split(lent)
-    lcat = jnp.concatenate([l_hi, l_lo], axis=1)
-    for k in range(NB):
-        w = w1bc[k]
-        hi, lo = split(gm1t * jnp.concatenate([w, w], axis=1))
-        da = fast_dot(lcat, jnp.concatenate([hi, hi], axis=0)) + fast_dot(l_hi, lo)
-        term = da * z_v[pl.ds(k * E, E), :]
-        q_v[...] = term if k == 0 else q_v[...] + term
 
     factor = -2.0 / (0.2 * ROOT)
 
@@ -456,6 +483,7 @@
     ]
     for copy in fifth:
         copy.start()
+    radial_grad(range(NB), (0, A))
     pulls = lax.fori_loop(0, A // 16, force_rows(0), pulls, unroll=UNROLL)
     centre = [jnp.sum(v, axis=0, keepdims=True) for v in pulls]
     lower = jnp.concatenate(centre[0::2], axis=0) - row_sums(0) - jnp.where(low, l_end, 0.0)
@@ -510,11 +538,11 @@
             f32(6, H), f32(6, H), f32(6, H), f32(6, H), f32(6, H),
             i32(K, A), i32(K, H), f32(E, A), f32(E, H), f32(4, E, H), f32(4, E, H), f32(8, A), f32(8, H),
             f32(NB, CH, H), f32(CH, CH),
-            b16(2 * CH, CH), b16(CH, CH), b16(2 * NB, 2 * CH), b16(2 * CH, CH), b16(CH, CH),
-            b16(2 * CH, CH), b16(CH, CH), b16(CH, 2 * CH), b16(CH, 2 * CH),
-            f32(E, CH), f32(E, CH), b16(NB * E, A), b16(NB * E, A), f32(NB * E, A), f32(NB * E, H),
-            f32(E, A), f32(E, H), b16(2 * CH, NB * E), f32(E, A),
-            f32(2 * NB, E), f32(3, E, H), f32(3, E, H),
+            b16(2 * CH, 2 * CH), b16(2 * NB, 2 * CH), b16(2 * CH, 2 * CH), b16(2 * CH, 2 * CH),
+            b16(CH, 2 * CH), b16(CH, 2 * CH),
+            f32(E, CH), f32(E, CH), b16(E, NB * A), b16(E, NB * A), f32(NB * E, A), f32(NB * E, H),
+            f32(E, A), f32(E, H), b16(NB * A, 2 * CH), f32(E, A),
+            b16(CH, 4 * H), f32(2 * NB, E), f32(3, E, H), f32(3, E, H),
             f32(6, H), f32(6, H), f32(3, H), f32(3, H), f32(6, H), f32(6, H), f32(3, H), f32(3, H),
             f32(6, H), f32(nb, 6, H),
             dma((10,)), dma((nb,)), dma((nb,)), dma((12,)), dma((12,)), dma((4,)), dma((4,)), dma((4,)), dma((4,)),

time: 38.5 us -> 37.6 us (0.977)
  Pallas kernels: 37.7 us -> 36.9 us
    pallas_call x1, Pallas kernels: 37.7 us -> 36.9 us  [on_device(): pl.pallas_call(functools.partial(kernel, nb, ns, own), out_shape=jax.Shap...]
where the time goes in v3:
time: 37.6 us; the launch traced here: 37.5 us
  Pallas kernels  36.9 us (98%)
  local copies, waits for them, and re-layouts  0.6 us (2%)
    pallas_call x1, Pallas kernels, on_device(): pl.pallas_call(functools.partial(kernel, nb, ns, own), out_shape=jax.Shap...  36.9 us

profile of v3, /device:TPU:24, one launch (start us, length us, event | category | flops | bytes accessed | tf_op | source)
XLA Modules:
  0.0 37.5 jit_solution(10700242514836248942)
XLA Ops:
  0.0 36.9 %shard_map.100 = f32[3,4,256]{2,1,0:T(4,128)S(1)} custom-call(f32[3,4,256]{2,1,0:T(4,128)} %bitcast.7, s32[2,128]{1,0:T(2,128)} %bitcast.8, s32[32,256]{1,0:T(8,128)} %nbr_h.1, s32[2,128]{1,0:T(2,128)} %bitcast.9, s32[1,128]{1,0:T(1,128)} %bitcast.10, f32[2,128]{1,0:T(2,128)} %emb_h.1, f32[2,8,128]{2,1,0:T(8,128)} %wr_h.1, f32[2,128,128]{2,1,0:T(8,128)} %wm_h.1, ...), custom_call_target="tpu_custom_call" | custom-call | tf_op jit(solution)/shard_map/pallas_call | solution.py:551
  36.9 0.6 %copy.12 = f32[4,3,256]{2,0,1:T(4,128)} copy(f32[4,3,256]{2,0,1:T(4,128)S(1)} %bitcast.6) | data formatting | bytes 24576

commit v4 on v3

--- a/solution.py
+++ b/solution.py
@@ -69,6 +69,16 @@
     return both[:, :CH] + both[:, CH:]
 
 
+def beside(w):
+    hi, lo = split(w)
+    return jnp.concatenate([hi, lo], axis=1)
+
+
+def left_dot(w, a):
+    hi, lo = split(a)
+    return fast_dot(w, jnp.concatenate([hi, hi], axis=0)) + fast_dot(w[:, :CH], lo)
+
+
 def fast_dot_nt(a, b):
     return lax.dot_general(a, b, (((1,), (1,)), ((), ())), preferred_element_type=F32)
 
@@ -82,7 +92,7 @@
     spc_r, snd_r, cnt_r, nbr_r, spc_l, snd_l, cnt_l, nbr_l, spc_rr, snd_rr, spc_ll, snd_ll,
     red_v, red_r, red_l, red_rr, red_ll,
     idx_v, idx_g, cnt_mat, cnt_gh, gb, ggb, cen, ceng, w1bc, wocol,
-    p0r_w, p0_cat, wm_w, wmt_w, wu_cat, wut_cat,
+    p0rt_cat, p0_cat, wmt_cat, wmt_w, wu_cat, wut_cat,
     h0_v, slope0, ah_v, al_v, z_v, zg_v, rinv_v, rinvg_v, gs_v, q_v,
     pick_v, dbs, fold_v, foldg_v, tx_r, tx_l, tx_rr, tx_ll, rx_r, rx_l, rx_rr, rx_ll, tx6, rx6,
     load_sem, s1, r1, sa, ra, s2, r2, s5, r5, s6, r6,
@@ -185,18 +195,17 @@
     p0 = exact_dot(rows0, wu_v[0])
     p0_hi, p0_lo = split(p0)
     p0_cat[...] = jnp.concatenate([p0_hi, p0_lo], axis=1)
-    p0r_w[...] = wide(jnp.concatenate(
-        [jnp.broadcast_to(p0[j : j + 1, :], (8, CH)) for j in range(2 * NB)], axis=0))
+    p0rt_cat[...] = beside(jnp.transpose(jnp.concatenate(
+        [jnp.broadcast_to(p0[j : j + 1, :], (8, CH)) for j in range(2 * NB)], axis=0)))
     w1 = wr_v[1] * scale
     w1t = jnp.transpose(jnp.concatenate([w1, jnp.zeros((CH - NB, CH), F32)], axis=0))
     for k in range(NB):
         w1bc[k] = jnp.broadcast_to(w1t[:, k : k + 1], (CH, H))
-    wm_w[...] = wide(wm_v[1])
-    wmt_w[...] = wide(jnp.transpose(wm_v[1]))
-    hi, lo = split(wu_v[1])
-    wu_cat[...] = jnp.concatenate([hi, lo], axis=1)
-    hi, lo = split(jnp.transpose(wu_v[1]))
-    wut_cat[...] = jnp.concatenate([hi, lo], axis=1)
+    wm_turned = jnp.transpose(wm_v[1])
+    wmt_cat[...] = beside(wm_turned)
+    wmt_w[...] = wide(wm_turned)
+    wu_cat[...] = beside(wu_v[1])
+    wut_cat[...] = beside(jnp.transpose(wu_v[1]))
     wocol[...] = jnp.transpose(jnp.broadcast_to(wo_v[...], (CH, CH)))
 
     lane = lax.broadcasted_iota(jnp.int32, (1, H), 1)
@@ -240,10 +249,9 @@
     kind_rg = jnp.where(low, spc_rr[0:1, :].astype(F32), kind_own[1:2])
     kind_lg = jnp.where(low, kind_own[0:1], spc_ll[1:2, :].astype(F32))
     zrest = jnp.zeros((CH - 4, H), F32)
-    z3 = jnp.zeros((3, H), F32)
+    kinds = [jnp.transpose(jnp.broadcast_to(emb_v[t : t + 1, :], (H, CH))) for t in range(2)]
     for part, kind in enumerate((kind_own[0:1], kind_own[1:2], kind_gh)):
-        kcol = jnp.transpose(jnp.concatenate([z3, kind, zrest], axis=0))
-        h0_v[pl.ds(part * H, H), :] = jnp.where(kcol[:, 3:4] > 0.5, emb_v[1:2, :], emb_v[0:1, :])
+        h0_v[:, pl.ds(part * H, H)] = jnp.where(kind > 0.5, kinds[1], kinds[0])
     cen[...] = jnp.concatenate(
         [jnp.concatenate([red[0:3], red[3:6]], axis=1), jnp.zeros((5, A), F32)], axis=0)
 
@@ -351,12 +359,10 @@
     stacked = jnp.concatenate(
         [jnp.concatenate(sums[0::2], axis=0), jnp.concatenate(sums[1::2], axis=0),
          jnp.concatenate(gsums, axis=0)], axis=1)
-    u0 = wide_dot(jnp.transpose(stacked), p0r_w[...])
+    u0 = left_dot(p0rt_cat[...], stacked)
     sig0 = 1.0 / (1.0 + jnp.exp(-u0))
-    slope0[...] = sig0 * (1.0 + u0 * (1.0 - sig0))
-    lent = wide_dot(h0_v[...] + u0 * sig0, wm_w[...])
-
-    lt = jnp.transpose(lent)
+    lt = left_dot(wmt_cat[...], h0_v[...] + u0 * sig0)
+
     message = None
     for k in range(0, NB, 2):
         parts = [split(lt * jnp.concatenate([w1bc[m]] * 3, axis=1)) for m in (k, k + 1)]
@@ -366,14 +372,14 @@
         both = fast_dot(jnp.concatenate([hi, lo], axis=0), a_hi)
         term = both[:CH] + both[CH:] + fast_dot(hi, a_lo)
         message = term if message is None else message + term
-    hi, lo = split(message)
-    wut = wut_cat[...]
-    u1 = fast_dot(wut, jnp.concatenate([hi, hi], axis=0)) + fast_dot(wut[:, :CH], lo)
+    slope0[...] = jnp.transpose(sig0 * (1.0 + u0 * (1.0 - sig0)))
+    lent = jnp.transpose(lt)
+    l_hi, l_lo = split(lent)
+    lcat = jnp.concatenate([l_hi, l_lo], axis=1)
+    u1 = left_dot(wut_cat[...], message)
     sig1 = 1.0 / (1.0 + jnp.exp(-u1))
     wo2 = jnp.concatenate([wocol[...], wocol[...]], axis=1)
-    hi, lo = split(wo2 * (sig1 * (1.0 + u1 * (1.0 - sig1))))
-    wu = wu_cat[...]
-    gm1t = fast_dot(wu, jnp.concatenate([hi, hi], axis=0)) + fast_dot(wu[:, :CH], lo)
+    gm1t = left_dot(wu_cat[...], wo2 * (sig1 * (1.0 + u1 * (1.0 - sig1))))
     gm1 = jnp.transpose(gm1t)
     for k in range(NB):
         hi, lo = split(gm1 * w1[k : k + 1, :])
@@ -382,8 +388,6 @@
     both = fast_dot(ah_v[...], gs_v[...])
     both = both + fast_dot(al_v[...], gs_v[...])
     dl = both[:, :CH] + both[:, CH:]
-    l_hi, l_lo = split(lent)
-    lcat = jnp.concatenate([l_hi, l_lo], axis=1)
 
     def radial_grad(ks, rows):
         for k in ks:
@@ -538,9 +542,9 @@
             f32(6, H), f32(6, H), f32(6, H), f32(6, H), f32(6, H),
             i32(K, A), i32(K, H), f32(E, A), f32(E, H), f32(4, E, H), f32(4, E, H), f32(8, A), f32(8, H),
             f32(NB, CH, H), f32(CH, CH),
-            b16(2 * CH, 2 * CH), b16(2 * NB, 2 * CH), b16(2 * CH, 2 * CH), b16(2 * CH, 2 * CH),
+            b16(CH, 2 * CH), b16(2 * NB, 2 * CH), b16(CH, 2 * CH), b16(2 * CH, 2 * CH),
             b16(CH, 2 * CH), b16(CH, 2 * CH),
-            f32(E, CH), f32(E, CH), b16(E, NB * A), b16(E, NB * A), f32(NB * E, A), f32(NB * E, H),
+            f32(CH, E), f32(E, CH), b16(E, NB * A), b16(E, NB * A), f32(NB * E, A), f32(NB * E, H),
             f32(E, A), f32(E, H), b16(NB * A, 2 * CH), f32(E, A),
             b16(CH, 4 * H), f32(2 * NB, E), f32(3, E, H), f32(3, E, H),
             f32(6, H), f32(6, H), f32(3, H), f32(3, H), f32(6, H), f32(6, H), f32(3, H), f32(3, H),

time: 37.6 us -> 37.6 us (level)
  no operation moved by 1% of the time
where the time goes in v4:
time: 37.6 us; the launch traced here: 37.5 us
  Pallas kernels  36.9 us (98%)
  local copies, waits for them, and re-layouts  0.6 us (2%)
    pallas_call x1, Pallas kernels, on_device(): pl.pallas_call(functools.partial(kernel, nb, ns, own), out_shape=jax.Shap...  36.9 us

profile of v4, /device:TPU:24, one launch (start us, length us, event | category | flops | bytes accessed | tf_op | source)
XLA Modules:
  0.0 37.5 jit_solution(8410659001700524335)
XLA Ops:
  0.0 36.9 %shard_map.100 = f32[3,4,256]{2,1,0:T(4,128)S(1)} custom-call(f32[3,4,256]{2,1,0:T(4,128)} %bitcast.7, s32[2,128]{1,0:T(2,128)} %bitcast.8, s32[32,256]{1,0:T(8,128)} %nbr_h.1, s32[2,128]{1,0:T(2,128)} %bitcast.9, s32[1,128]{1,0:T(1,128)} %bitcast.10, f32[2,128]{1,0:T(2,128)} %emb_h.1, f32[2,8,128]{2,1,0:T(8,128)} %wr_h.1, f32[2,128,128]{2,1,0:T(8,128)} %wm_h.1, ...), custom_call_target="tpu_custom_call" | custom-call | tf_op jit(solution)/shard_map/pallas_call | solution.py:555
  36.9 0.6 %copy.12 = f32[4,3,256]{2,0,1:T(4,128)} copy(f32[4,3,256]{2,0,1:T(4,128)S(1)} %bitcast.6) | data formatting | bytes 24576

commit v5 on v4

--- a/solution.py
+++ b/solution.py
@@ -223,7 +223,7 @@
     red_v[...] = red
     second = [
         side_copy(red_v, dst, s2.at[i], r2.at[i], side)
-        for i, (dst, side) in enumerate(((red_r, left), (red_l, right), (red_rr, left2), (red_ll, right2)))
+        for i, (dst, side) in enumerate(((red_rr, left2), (red_ll, right2), (red_r, left), (red_l, right)))
     ]
     for copy in second:
         copy.start()
@@ -470,22 +470,24 @@
 
     gpulls = tuple(jnp.zeros((8, H), F32) for _ in range(3))
     gpulls = lax.fori_loop(0, E // 32, ghost_force, gpulls, unroll=UNROLL)
+    r_end, l_end = ghost_sums(2 * H)
+    tx_rr[...] = r_end
+    tx_ll[...] = l_end
+    r_low, l_low = ghost_sums(0)
+    fifth = [
+        side_copy(src, dst, s5.at[i], r5.at[i], side)
+        for i, (src, dst, side) in enumerate((
+            (tx_rr, rx_ll, right2), (tx_ll, rx_rr, left2), (tx_r, rx_l, right), (tx_l, rx_r, left)))
+    ]
+    for copy in fifth[:2]:
+        copy.start()
     pulls = tuple(jnp.zeros((8, H), F32) for _ in range(6))
     pulls = lax.fori_loop(0, 2 * G // 16, force_rows(A), pulls, unroll=UNROLL)
     lent_pull = row_sums(A) - jnp.concatenate([jnp.sum(v, axis=0, keepdims=True) for v in gpulls], axis=0)
-    r_low, l_low = ghost_sums(0)
     r_high, l_high = ghost_sums(H)
-    r_end, l_end = ghost_sums(2 * H)
     tx_r[...] = jnp.concatenate([r_low + jnp.where(low, lent_pull, 0.0), r_high], axis=0)
     tx_l[...] = jnp.concatenate([l_low, l_high + jnp.where(low, 0.0, lent_pull)], axis=0)
-    tx_rr[...] = r_end
-    tx_ll[...] = l_end
-    fifth = [
-        side_copy(src, dst, s5.at[i], r5.at[i], side)
-        for i, (src, dst, side) in enumerate((
-            (tx_r, rx_l, right), (tx_l, rx_r, left), (tx_rr, rx_ll, right2), (tx_ll, rx_rr, left2)))
-    ]
-    for copy in fifth:
+    for copy in fifth[2:]:
         copy.start()
     radial_grad(range(NB), (0, A))
     pulls = lax.fori_loop(0, A // 16, force_rows(0), pulls, unroll=UNROLL)
@@ -501,6 +503,8 @@
     last = {lag: bead_copy(tx6, rx6.at[lag], s6.at[lag], r6.at[lag], lag) for lag in lags}
     for lag in lags:
         last[lag].start()
+    for copy in list(first.values()) + aux + second + fifth:
+        copy.wait_send()
     ratio = beads / reduced
     totals = [ratio * table_value(-j, beads, reduced) * pull for j in range(own)]
     for lag in reversed(lags):
@@ -513,7 +517,7 @@
             row = 3 * half + c
             out_ref[c, :, half * H : half * H + H] = jnp.concatenate(
                 [totals[j][row : row + 1] for j in range(own)], axis=0)
-    for copy in list(first.values()) + aux + second + fifth + list(last.values()):
+    for copy in last.values():
         copy.wait_send()
 
 

time: 37.6 us -> 37.2 us (0.989)
  Pallas kernels: 36.9 us -> 36.5 us
    pallas_call x1, Pallas kernels: 36.9 us -> 36.5 us  [on_device(): pl.pallas_call(functools.partial(kernel, nb, ns, own), out_shape=jax.Shap...]
where the time goes in v5:
time: 37.2 us; the launch traced here: 37.1 us
  Pallas kernels  36.5 us (98%)
  local copies, waits for them, and re-layouts  0.6 us (2%)
    pallas_call x1, Pallas kernels, on_device(): pl.pallas_call(functools.partial(kernel, nb, ns, own), out_shape=jax.Shap...  36.5 us

profile of v5, /device:TPU:24, one launch (start us, length us, event | category | flops | bytes accessed | tf_op | source)
XLA Modules:
  0.0 37.1 jit_solution(7624728925040022775)
XLA Ops:
  0.0 36.5 %shard_map.100 = f32[3,4,256]{2,1,0:T(4,128)S(1)} custom-call(f32[3,4,256]{2,1,0:T(4,128)} %bitcast.7, s32[2,128]{1,0:T(2,128)} %bitcast.8, s32[32,256]{1,0:T(8,128)} %nbr_h.1, s32[2,128]{1,0:T(2,128)} %bitcast.9, s32[1,128]{1,0:T(1,128)} %bitcast.10, f32[2,128]{1,0:T(2,128)} %emb_h.1, f32[2,8,128]{2,1,0:T(8,128)} %wr_h.1, f32[2,128,128]{2,1,0:T(8,128)} %wm_h.1, ...), custom_call_target="tpu_custom_call" | custom-call | tf_op jit(solution)/shard_map/pallas_call | solution.py:559
  36.5 0.6 %copy.12 = f32[4,3,256]{2,0,1:T(4,128)} copy(f32[4,3,256]{2,0,1:T(4,128)S(1)} %bitcast.6) | data formatting | bytes 24576

commit v6 on v5

--- a/solution.py
+++ b/solution.py
@@ -24,7 +24,7 @@
 STEP = ROOT / 0.2
 CENTERS = tuple(STEP * 1.5 * b / (NB - 1) for b in range(NB))
 FLOOR = 0.01
-UNROLL = 2
+UNROLL = 4
 
 
 def by_distance(nb):

time: 37.2 us -> 37.2 us (level)
  no operation moved by 1% of the time
where the time goes in v6:
time: 37.2 us; the launch traced here: 37 us
  Pallas kernels  36.4 us (98%)
  local copies, waits for them, and re-layouts  0.6 us (2%)
    pallas_call x1, Pallas kernels, on_device(): pl.pallas_call(functools.partial(kernel, nb, ns, own), out_shape=jax.Shap...  36.4 us

profile of v6, /device:TPU:24, one launch (start us, length us, event | category | flops | bytes accessed | tf_op | source)
XLA Modules:
  0.0 37.0 jit_solution(3908362006228918246)
XLA Ops:
  0.0 36.4 %shard_map.100 = f32[3,4,256]{2,1,0:T(4,128)S(1)} custom-call(f32[3,4,256]{2,1,0:T(4,128)} %bitcast.7, s32[2,128]{1,0:T(2,128)} %bitcast.8, s32[32,256]{1,0:T(8,128)} %nbr_h.1, s32[2,128]{1,0:T(2,128)} %bitcast.9, s32[1,128]{1,0:T(1,128)} %bitcast.10, f32[2,128]{1,0:T(2,128)} %emb_h.1, f32[2,8,128]{2,1,0:T(8,128)} %wr_h.1, f32[2,128,128]{2,1,0:T(8,128)} %wm_h.1, ...), custom_call_target="tpu_custom_call" | custom-call | tf_op jit(solution)/shard_map/pallas_call | solution.py:559
  36.4 0.6 %copy.12 = f32[4,3,256]{2,0,1:T(4,128)} copy(f32[4,3,256]{2,0,1:T(4,128)S(1)} %bitcast.6) | data formatting | bytes 24576
